TPU v7x, 8 devices: a whole 2x2x1 slice. The times are simulated.
8 devices in a mesh: dp: 1 (over z), tp: 8 (over y, x, core).
Axes of the slice: x: 2, y: 2, z: 1, core: 2. Of those that a mesh axis runs over, the one named last changes fastest.
Arguments:
- x: bfloat16 [1, 2048, 2048], P('dp', 'tp')
- ln1_gamma: float32 [2048], replicated
- ln1_beta: float32 [2048], replicated
- w_qkv: bfloat16 [2048, 16, 3, 128], P(None, 'tp')
- b_qkv: float32 [16, 3, 128], P('tp')
- w_out: bfloat16 [2048, 2048], P('tp')
- b_out: float32 [2048], replicated
- ln2_gamma: float32 [2048], replicated
- ln2_beta: float32 [2048], replicated
- w_up: bfloat16 [2048, 8192], P(None, 'tp')
- b_up: float32 [8192], P('tp')
- w_down: bfloat16 [8192, 2048], P('tp')
- b_down: float32 [2048], replicated
- grad_y: bfloat16 [1, 2048, 2048], P('dp', 'tp')
Outputs:
- output 1: bfloat16 [1, 2048, 2048], P('dp', 'tp')
- output 2: bfloat16 [1, 2048, 2048], P('dp', 'tp')
- output 3: float32 [2048], P('dp')
- output 4: float32 [2048], P('dp')
- output 5: bfloat16 [2048, 16, 3, 128], P('dp', 'tp')
- output 6: float32 [16, 3, 128], P(('dp', 'tp'))
- output 7: bfloat16 [2048, 2048], P(('dp', 'tp'))
- output 8: float32 [2048], P('dp')
- output 9: float32 [2048], P('dp')
- output 10: float32 [2048], P('dp')
- output 11: bfloat16 [2048, 8192], P('dp', 'tp')
- output 12: float32 [8192], P(('dp', 'tp'))
- output 13: bfloat16 [8192, 2048], P(('dp', 'tp'))
- output 14: float32 [2048], P('dp')
All inputs are finite; a program needn't handle non-finite values.
Results may differ from a plain program's by a relative error of at most 0.02.
Values are sent between devices in bfloat16 or wider.
A program may use at most 1 GiB of HBM per device.

v0:
```python
import math
import jax
import jax.numpy as jnp
from jax import lax
from jax.sharding import PartitionSpec as P

EPS = 1e-5
MASK_VALUE = -1e30


def alibi_slopes(n_heads):
    closest = 2 ** int(math.floor(math.log2(n_heads)))
    base_ratio = 2.0 ** (-8.0 / closest)
    extra_ratio = 2.0 ** (-4.0 / closest)
    remaining = min(closest, n_heads - closest)
    slopes = [base_ratio ** (i + 1) for i in range(closest)]
    slopes = slopes + [extra_ratio ** (2 * i + 1) for i in range(remaining)]
    return jnp.array(slopes, dtype=jnp.float32)


def layer_norm(values, ln_gain, ln_bias):
    row_mean = jnp.mean(values, axis=-1, keepdims=True)
    centered = values - row_mean
    variance = jnp.mean(centered * centered, axis=-1, keepdims=True)
    return centered * lax.rsqrt(variance + EPS) * ln_gain + ln_bias


def gelu_tanh(values):
    return jax.nn.gelu(values, approximate=True)


def seq_gather(values):
    return lax.all_gather(values, 'tp', axis=1, tiled=True)


def seq_reduce(values):
    return lax.psum_scatter(values, 'tp', scatter_dimension=1, tiled=True)


def solution(mesh):
    tp_size = mesh.shape['tp']

    def local_step(x, ln1_gamma, ln1_beta, w_qkv, b_qkv, w_out, b_out, ln2_gamma, ln2_beta, w_up, b_up, w_down, b_down, grad_y):
        batch_size, seq_local = x.shape[0], x.shape[1]
        local_heads, head_size = w_qkv.shape[1], w_qkv.shape[3]
        seq_full = seq_local * tp_size
        score_scale = head_size ** -0.5
        tp_index = lax.axis_index('tp')
        slopes = lax.dynamic_slice_in_dim(alibi_slopes(local_heads * tp_size), tp_index * local_heads, local_heads)
        positions = jnp.arange(seq_full)
        causal = positions[None, :] <= positions[:, None]
        alibi_bias = slopes[:, None] * positions.astype(jnp.float32)[None, :]

        x_f = x.astype(jnp.float32)
        h_full = seq_gather(layer_norm(x_f, ln1_gamma, ln1_beta).astype(jnp.bfloat16))
        qkv_vals = (jnp.einsum('bsd,dhte->bshte', h_full, w_qkv, preferred_element_type=jnp.float32) + b_qkv).astype(jnp.bfloat16)
        q_heads = qkv_vals[:, :, :, 0]
        k_heads = qkv_vals[:, :, :, 1]
        v_heads = qkv_vals[:, :, :, 2]
        scores = jnp.einsum('bihe,bjhe->bhij', q_heads, k_heads, preferred_element_type=jnp.float32) * score_scale + alibi_bias[None, :, None, :]
        prob_f = jax.nn.softmax(jnp.where(causal, scores, MASK_VALUE), axis=-1)
        prob_bf = prob_f.astype(jnp.bfloat16)
        context = jnp.einsum('bhij,bjhe->bihe', prob_bf, v_heads, preferred_element_type=jnp.float32).astype(jnp.bfloat16)
        context_flat = context.reshape(batch_size, seq_full, local_heads * head_size)
        attn_out = seq_reduce(jnp.einsum('bsc,cd->bsd', context_flat, w_out, preferred_element_type=jnp.float32).astype(jnp.bfloat16))
        x_mid = x_f + attn_out.astype(jnp.float32) + b_out
        g_full = seq_gather(layer_norm(x_mid, ln2_gamma, ln2_beta).astype(jnp.bfloat16))
        pre_act = jnp.einsum('bsd,df->bsf', g_full, w_up, preferred_element_type=jnp.float32) + b_up
        activated = gelu_tanh(pre_act).astype(jnp.bfloat16)
        mlp_out = seq_reduce(jnp.einsum('bsf,fd->bsd', activated, w_down, preferred_element_type=jnp.float32).astype(jnp.bfloat16))
        y = (x_mid + mlp_out.astype(jnp.float32) + b_down).astype(jnp.bfloat16)

        grad_y_f = grad_y.astype(jnp.float32)
        grad_b_down = lax.psum(jnp.sum(grad_y_f, axis=(0, 1)), 'tp')
        grad_m_full = seq_gather(grad_y)
        grad_w_down = jnp.einsum('bsf,bsd->fd', activated, grad_m_full, preferred_element_type=jnp.float32).astype(jnp.bfloat16)
        grad_act = jnp.einsum('bsd,fd->bsf', grad_m_full, w_down, preferred_element_type=jnp.float32).astype(jnp.bfloat16)
        _, gelu_pullback = jax.vjp(gelu_tanh, pre_act)
        grad_pre = gelu_pullback(grad_act.astype(jnp.float32))[0]
        grad_b_up = jnp.sum(grad_pre, axis=(0, 1))
        grad_pre_bf = grad_pre.astype(jnp.bfloat16)
        grad_w_up = jnp.einsum('bsd,bsf->df', g_full, grad_pre_bf, preferred_element_type=jnp.float32).astype(jnp.bfloat16)
        grad_g = seq_reduce(jnp.einsum('bsf,df->bsd', grad_pre_bf, w_up, preferred_element_type=jnp.float32).astype(jnp.bfloat16))
        _, ln2_pullback = jax.vjp(layer_norm, x_mid, ln2_gamma, ln2_beta)
        grad_mid_ln, grad_ln2_gamma, grad_ln2_beta = ln2_pullback(grad_g.astype(jnp.float32))
        grad_ln2_gamma = lax.psum(grad_ln2_gamma, 'tp')
        grad_ln2_beta = lax.psum(grad_ln2_beta, 'tp')
        grad_mid = grad_y_f + grad_mid_ln
        grad_b_out = lax.psum(jnp.sum(grad_mid, axis=(0, 1)), 'tp')
        grad_attn_full = seq_gather(grad_mid.astype(jnp.bfloat16))
        grad_w_out = jnp.einsum('bsc,bsd->cd', context_flat, grad_attn_full, preferred_element_type=jnp.float32).astype(jnp.bfloat16)
        grad_context = jnp.einsum('bsd,cd->bsc', grad_attn_full, w_out, preferred_element_type=jnp.float32).astype(jnp.bfloat16)
        grad_context = grad_context.reshape(batch_size, seq_full, local_heads, head_size)
        grad_prob = jnp.einsum('bihe,bjhe->bhij', grad_context, v_heads, preferred_element_type=jnp.float32).astype(jnp.bfloat16).astype(jnp.float32)
        grad_v = jnp.einsum('bhij,bihe->bjhe', prob_bf, grad_context, preferred_element_type=jnp.float32).astype(jnp.bfloat16)
        grad_scores = prob_f * (grad_prob - jnp.sum(grad_prob * prob_f, axis=-1, keepdims=True))
        grad_scores_bf = grad_scores.astype(jnp.bfloat16)
        grad_q = (jnp.einsum('bhij,bjhe->bihe', grad_scores_bf, k_heads, preferred_element_type=jnp.float32) * score_scale).astype(jnp.bfloat16)
        grad_k = (jnp.einsum('bhij,bihe->bjhe', grad_scores_bf, q_heads, preferred_element_type=jnp.float32) * score_scale).astype(jnp.bfloat16)
        grad_qkv = jnp.stack([grad_q, grad_k, grad_v], axis=3)
        grad_b_qkv = jnp.sum(grad_qkv, axis=(0, 1), dtype=jnp.float32)
        grad_w_qkv = jnp.einsum('bsd,bshte->dhte', h_full, grad_qkv, preferred_element_type=jnp.float32).astype(jnp.bfloat16)
        grad_h = seq_reduce(jnp.einsum('bshte,dhte->bsd', grad_qkv, w_qkv, preferred_element_type=jnp.float32).astype(jnp.bfloat16))
        _, ln1_pullback = jax.vjp(layer_norm, x_f, ln1_gamma, ln1_beta)
        grad_x_ln, grad_ln1_gamma, grad_ln1_beta = ln1_pullback(grad_h.astype(jnp.float32))
        grad_ln1_gamma = lax.psum(grad_ln1_gamma, 'tp')
        grad_ln1_beta = lax.psum(grad_ln1_beta, 'tp')
        grad_x = (grad_mid + grad_x_ln).astype(jnp.bfloat16)
        return (y, grad_x, grad_ln1_gamma, grad_ln1_beta, grad_w_qkv, grad_b_qkv, grad_w_out, grad_b_out,
                grad_ln2_gamma, grad_ln2_beta, grad_w_up, grad_b_up, grad_w_down, grad_b_down)

    row_spec = P('dp', 'tp', None)
    in_specs = (row_spec, P(), P(), P(None, 'tp', None, None), P('tp', None, None), P('tp', None), P(), P(), P(),
                P(None, 'tp'), P('tp'), P('tp', None), P(), row_spec)
    out_specs = (row_spec, row_spec, P('dp'), P('dp'), P('dp', 'tp', None, None), P(('dp', 'tp'), None, None),
                 P(('dp', 'tp'), None), P('dp'), P('dp'), P('dp'), P('dp', 'tp'), P(('dp', 'tp')), P(('dp', 'tp'), None), P('dp'))
    return jax.shard_map(local_step, mesh=mesh, in_specs=in_specs, out_specs=out_specs, check_vma=False)
```

profile of v0, /device:TPU:0, one launch (start us, length us, event | category | flops | bytes accessed | tf_op | source)
XLA Modules:
  0.0 708.6 jit_solution(18034627335505824028)
XLA Ops:
  18.7 46.9 %all-gather.5.cloned.1.call-done = bf16[1,2048,2048]{2,1,0:T(8,128)(2,1)} async-done(((bf16[1,256,2048]{2,1,0:T(8,128)(2,1)}), bf16[1,2048,2048]{2,1,0:T(8,128)(2,1)}) %all-gather.5.cloned.1.call-update) | async-done | bytes 8388624 | tf_op jit(solution)/shard_map/all_gather | solution.py:33
  65.7 10.2 %fusion.58 = bf16[1,2048,2,3,128]{4,1,3,2,0:T(8,128)(2,1)} fusion(f32[2,3,128]{2,1,0:T(4,128)S(1)} %copy.30, bf16[1,2048,2048]{2,1,0:T(8,128)(2,1)} %all-gather.5.cloned.1.call-done, bf16[2048,2,3,128]{3,1,2,0:T(2,128)(2,1)S(1)} %copy-done), kind=kOutput, calls=%fused_computation.77 | convolution fusion | flops 6445596672 | bytes 14683136 | tf_op jit(solution)/shard_map/bsd,dhte->bshte/dot_general | solution.py:56
  75.8 19.4 %fusion.109 = (f32[2,2048]{1,0:T(2,128)S(1)}, f32[2,2048,2048]{1,2,0:T(8,128)}) fusion(f32[2,2048]{1,0:T(2,128)S(1)} %broadcast_multiply_fusion, pred[2048,2048]{0,1:T(8,128)(4,1)} %iota_compare_fusion, bf16[1,2048,2,3,128]{4,1,3,2,0:T(8,128)(2,1)} %fusion.58), kind=kOutput, calls=%fused_computation.137 | convolution fusion | flops 2189428736 | bytes 39878656 | tf_op jit(solution)/shard_map/sub | solution.py:61
  95.3 12.4 %fusion.67 = bf16[2,128,2048]{2,1,0:T(8,128)(2,1)S(1)} fusion(bf16[1,2048,2,3,128]{4,1,3,2,0:T(8,128)(2,1)} %fusion.58, f32[2,2048,2048]{1,2,0:T(8,128)} %get-tuple-element.47, f32[2,2048]{1,0:T(2,128)S(1)} %get-tuple-element.46), kind=kOutput, calls=%fused_computation.88 | convolution fusion | flops 2164785152 | bytes 35667968 | tf_op jit(solution)/shard_map/bhij,bjhe->bihe/dot_general | solution.py:63
  114.5 62.1 %reduce-scatter.5.cloned.1.call-done = bf16[1,256,2048]{2,1,0:T(8,128)(2,1)} async-done(((bf16[1,2048,2048]{2,1,0:T(8,128)(2,1)}), bf16[1,256,2048]{2,1,0:T(8,128)(2,1)}) %reduce-scatter.5.cloned.1.call-update) | async-done | bytes 1048592 | tf_op jit(solution)/shard_map/reduce_scatter | solution.py:37
  183.2 47.8 %all-gather.7.cloned.1.call-done = bf16[1,2048,2048]{2,1,0:T(8,128)(2,1)} async-done(((bf16[1,256,2048]{2,1,0:T(8,128)(2,1)}), bf16[1,2048,2048]{2,1,0:T(8,128)(2,1)}) %all-gather.7.cloned.1.call-update) | async-done | bytes 8388624 | tf_op jit(solution)/shard_map/all_gather | solution.py:33
  231.1 14.4 %fusion.32 = f32[2048,1024]{1,0:T(8,128)} fusion(bf16[2048,1024]{1,0:T(8,128)(2,1)} %param.24, bf16[1,2048,2048]{2,1,0:T(8,128)(2,1)} %all-gather.7.cloned.1.call-done), kind=kOutput, calls=%fused_computation.44 | convolution fusion | flops 8589934592 | bytes 20971520 | tf_op jit(solution)/shard_map/bsd,df->bsf/dot_general | solution.py:68
  245.5 35.6 %all-gather.9.cloned.1.call-done = bf16[1,2048,2048]{2,1,0:T(8,128)(2,1)} async-done(((bf16[1,256,2048]{2,1,0:T(8,128)(2,1)}), bf16[1,2048,2048]{2,1,0:T(8,128)(2,1)}) %all-gather.9.cloned.1.call-update) | async-done | bytes 8388624 | tf_op jit(solution)/shard_map/all_gather | solution.py:33
  281.1 20.8 %fusion.110 = (f32[1024]{0:T(1024)}, bf16[2048,1024]{1,0:T(8,128)(2,1)S(1)}) fusion(f32[2048,1024]{1,0:T(8,128)} %fusion.32, f32[1024]{0:T(1024)S(1)} %copy-done.30, bf16[1024,2048]{1,0:T(8,128)(2,1)} %param.26, bf16[1,2048,2048]{2,1,0:T(8,128)(2,1)} %all-gather.9.cloned.1.call-done), kind=kOutput, calls=%fused_computation.138 | convolution fusion | flops 8640265216 | bytes 25174016 | tf_op jit(solution)/shard_map/bsd,fd->bsf/dot_general | solution.py:77
  304.0 11.1 %convert_bitcast_fusion = bf16[1,2048,2048]{2,1,0:T(8,128)(2,1)} fusion(bf16[2048,1024]{1,0:T(8,128)(2,1)S(1)} %copy-done.29, bf16[2048,1024]{1,0:T(8,128)(2,1)S(1)} %get-tuple-element.51), kind=kOutput, calls=%fused_computation.46 | convolution fusion | flops 8594128896 | bytes 16777216 | tf_op jit(solution)/shard_map/bsf,df->bsd/dot_general | solution.py:83
  315.1 15.4 %convert_bitcast_fusion.1 = bf16[1,2048,2048]{2,1,0:T(8,128)(2,1)} fusion(bf16[1024,2048]{1,0:T(8,128)(2,1)} %param.26, f32[2048,1024]{1,0:T(8,128)} %fusion.32, f32[1024]{0:T(1024)S(1)} %copy-done.30), kind=kOutput, calls=%fused_computation.47 | convolution fusion | flops 8615100416 | bytes 20975616 | tf_op jit(solution)/shard_map/bsf,fd->bsd/dot_general | solution.py:70
  330.6 46.9 %reduce-scatter.9.cloned.1.call-done = bf16[1,256,2048]{2,1,0:T(8,128)(2,1)} async-done(((bf16[1,2048,2048]{2,1,0:T(8,128)(2,1)}), bf16[1,256,2048]{2,1,0:T(8,128)(2,1)}) %reduce-scatter.9.cloned.1.call-update) | async-done | bytes 1048592 | tf_op jit(solution)/shard_map/reduce_scatter | solution.py:37
  384.4 58.5 %reduce-scatter.7.cloned.1.call-done = bf16[1,256,2048]{2,1,0:T(8,128)(2,1)} async-done(((bf16[1,2048,2048]{2,1,0:T(8,128)(2,1)}), bf16[1,256,2048]{2,1,0:T(8,128)(2,1)}) %reduce-scatter.7.cloned.1.call-update) | async-done | bytes 1048592 | tf_op jit(solution)/shard_map/reduce_scatter | solution.py:37
  451.4 48.5 %all-gather.11.cloned.1.call-done = bf16[1,2048,2048]{2,1,0:T(8,128)(2,1)} async-done(((bf16[1,256,2048]{2,1,0:T(8,128)(2,1)}), bf16[1,2048,2048]{2,1,0:T(8,128)(2,1)}) %all-gather.11.cloned.1.call-update) | async-done | bytes 8388624 | tf_op jit(solution)/shard_map/all_gather | solution.py:33
  506.8 15.1 %fusion.82 = bf16[1,2048,2,1,128]{1,4,2,3,0:T(8,128)(2,1)} fusion(bf16[2048,2,128]{0,2,1:T(8,128)(2,1)} %bitcast.138, f32[2,2048,2048]{1,2,0:T(8,128)} %get-tuple-element.47, f32[2,2048]{1,0:T(2,128)S(1)} %get-tuple-element.46), kind=kOutput, calls=%fused_computation.95 | convolution fusion | flops 2164785152 | bytes 35667968 | tf_op jit(solution)/shard_map/bhij,bihe->bjhe/dot_general | solution.py:95
  522.0 19.5 %fusion.1 = (f32[2,2048]{1,0:T(2,128)S(1)}, bf16[2,2048,2048]{1,2,0:T(8,128)(2,1)}) fusion(f32[2,2048,2048]{1,2,0:T(8,128)} %get-tuple-element.47, f32[2,2048]{1,0:T(2,128)S(1)} %get-tuple-element.46, bf16[2048,2,128]{0,2,1:T(8,128)(2,1)} %bitcast.139, bf16[1,2048,2,3,128]{4,1,3,2,0:T(8,128)(2,1)} %fusion.58), kind=kOutput, calls=%fused_computation.3 | convolution fusion | flops 2189422592 | bytes 52461568 | tf_op jit(solution)/shard_map/bihe,bjhe->bhij/dot_general | solution.py:94
  541.4 22.3 %fusion.3 = bf16[2,2048,2048]{1,2,0:T(8,128)(2,1)} fusion(bf16[2,2048,2048]{1,2,0:T(8,128)(2,1)} %get-tuple-element.49, f32[2,2048]{1,0:T(2,128)S(1)} %get-tuple-element.48, f32[2,2048,2048]{1,2,0:T(8,128)} %get-tuple-element.47, f32[2,2048]{1,0:T(2,128)S(1)} %get-tuple-element.46), kind=kLoop, calls=%fused_computation.5 | loop fusion | flops 41943040 | bytes 67141632 | tf_op jit(solution)/shard_map/convert_element_type | solution.py:97
  563.7 12.7 %fusion.85 = bf16[1,2048,2,1,128]{1,4,2,3,0:T(8,128)(2,1)} fusion(bf16[2,2048,2048]{1,2,0:T(8,128)(2,1)} %fusion.3, bf16[1,2048,2,3,128]{4,1,3,2,0:T(8,128)(2,1)} %fusion.58), kind=kOutput, calls=%fused_computation.96 | convolution fusion | flops 2148532224 | bytes 18874368 | tf_op jit(solution)/shard_map/bhij,bihe->bjhe/dot_general | solution.py:99
  586.1 9.4 %fusion.38 = bf16[1,2048,2048]{2,1,0:T(8,128)(2,1)} fusion(bf16[2048,2,3,128]{3,1,2,0:T(2,128)(2,1)S(1)} %copy-done, bf16[1,2048,2,1,128]{1,4,2,3,0:T(8,128)(2,1)S(1)} %copy-done.10, bf16[1,2048,2,1,128]{1,4,2,3,0:T(8,128)(2,1)S(1)} %copy-done.4, bf16[1,2048,2,1,128]{1,4,2,3,0:T(8,128)(2,1)S(1)} %fusion.86), kind=kOutput, calls=%fused_computation.54 | convolution fusion | flops 6449790976 | bytes 14680064 | tf_op jit(solution)/shard_map/bshte,dhte->bsd/dot_general | solution.py:103
  595.6 14.0 %fusion.46 = bf16[2048,1024]{1,0:T(8,128)(2,1)} fusion(bf16[1,2048,2048]{2,1,0:T(8,128)(2,1)} %all-gather.7.cloned.1.call-done, bf16[2048,1024]{1,0:T(8,128)(2,1)} %copy-done.32), kind=kOutput, calls=%fused_computation.59 | convolution fusion | flops 8592031744 | bytes 16777216 | tf_op jit(solution)/shard_map/bsd,bsf->df/dot_general | solution.py:82
  609.6 16.8 %fusion.43 = bf16[1024,2048]{1,0:T(8,128)(2,1)} fusion(bf16[1,2048,2048]{2,1,0:T(8,128)(2,1)} %all-gather.9.cloned.1.call-done, f32[2048,1024]{1,0:T(8,128)} %fusion.32, f32[1024]{0:T(1024)S(1)} %copy-done.30), kind=kOutput, calls=%fused_computation.58 | convolution fusion | flops 8613003264 | bytes 20975616 | tf_op jit(solution)/shard_map/bsf,bsd->fd/dot_general | solution.py:76
  626.4 9.4 %fusion.51 = bf16[2048,2,3,128]{3,0,2,1:T(8,128)(2,1)S(1)} fusion(bf16[1,2048,2048]{2,1,0:T(8,128)(2,1)} %all-gather.5.cloned.1.call-done, bf16[1,2048,2,1,128]{1,4,2,3,0:T(8,128)(2,1)S(1)} %copy-done.11, bf16[1,2048,2,1,128]{1,4,2,3,0:T(8,128)(2,1)S(1)} %copy-done.5, bf16[1,2048,2,1,128]{1,4,2,3,0:T(8,128)(2,1)S(1)} %copy-done.7), kind=kOutput, calls=%fused_computation.60 | convolution fusion | flops 6447169536 | bytes 14680064 | tf_op jit(solution)/shard_map/bsd,bshte->dhte/dot_general | solution.py:102
  635.8 28.7 %copy.43 = bf16[2048,2,3,128]{3,1,2,0:T(2,128)(2,1)} copy(bf16[2048,2,3,128]{3,0,2,1:T(8,128)(2,1)S(1)} %fusion.51) | data formatting | bytes 6291456
  673.9 23.5 %all-reduce = (f32[2048]{0:T(1024)}, f32[2048]{0:T(1024)}, f32[2048]{0:T(1024)}, f32[2048]{0:T(1024)}, f32[2048]{0:T(1024)}, /*index=5*/f32[2048]{0:T(1024)}) all-reduce(f32[2048]{0:T(1024)S(1)} %get-tuple-element.30, f32[2048]{0:T(1024)S(1)} %get-tuple-element.34, f32[2048]{0:T(1024)S(1)} %copy-done.20, ...), channel_id=1, replica_groups=mesh['dp'=1,'tp'=8] {'tp'}, use_global_device_ids=true, to_apply=%region_16.17 | all-reduce | flops 12288 | bytes 98304 | tf_op jit(solution)/shard_map/psum | solution.py:106
  (119 shorter events, 72.2 us)
Async XLA Ops:
  7.2 58.5 %copy-start = (bf16[2048,2,3,128]{3,1,2,0:T(2,128)(2,1)S(1)}, bf16[2048,2,3,128]{3,1,2,0:T(2,128)(2,1)}, u32[]{:S(2)}) copy-start(bf16[2048,2,3,128]{3,1,2,0:T(2,128)(2,1)} %param.18) | copy-start | bytes 9437188
  7.2 58.4 %all-gather.5.cloned.1.call-start = ((), (), s32[]{:S(2)}) async-start(), calls=%async_computation.4 | async-start | bytes 9437184 | tf_op jit(solution)/shard_map/all_gather | solution.py:33
  14.3 162.3 %reduce-scatter.5.cloned.1.call-start = ((), (), s32[]{:S(2)}) async-start(), calls=%async_computation.5 | async-start | bytes 9437184 | tf_op jit(solution)/shard_map/reduce_scatter | solution.py:37
  95.3 13.4 %copy-start.12 = (bf16[256,2048]{1,0:T(8,128)(2,1)S(1)}, bf16[256,2048]{1,0:T(8,128)(2,1)}, u32[]{:S(2)}) copy-start(bf16[256,2048]{1,0:T(8,128)(2,1)} %param.20) | copy-start | bytes 3145732
  114.2 62.4 %copy-start.13 = (f32[2048]{0:T(1024)S(1)}, f32[2048]{0:T(1024)}, u32[]{:S(2)}) copy-start(f32[2048]{0:T(1024)} %param.21) | copy-start | bytes 24580
  114.3 66.6 %copy-start.14 = (f32[2048]{0:T(1024)S(1)}, f32[2048]{0:T(1024)}, u32[]{:S(2)}) copy-start(f32[2048]{0:T(1024)} %param.22) | copy-start | bytes 24580
  114.3 66.6 %copy-start.26 = (f32[2048]{0:T(1024)S(1)}, f32[2048]{0:T(1024)}, u32[]{:S(2)}) copy-start(f32[2048]{0:T(1024)} %param.23) | copy-start | bytes 24580
  114.3 116.8 %all-gather.7.cloned.1.call-start = ((), (), s32[]{:S(2)}) async-start(), calls=%async_computation.6 | async-start | bytes 9437184 | tf_op jit(solution)/shard_map/all_gather | solution.py:33
  182.6 98.5 %all-gather.9.cloned.1.call-start = ((), (), s32[]{:S(2)}) async-start(), calls=%async_computation.8 | async-start | bytes 9437184 | tf_op jit(solution)/shard_map/all_gather | solution.py:33
  183.2 97.9 %copy-start.30 = (f32[1024]{0:T(1024)S(1)}, f32[1024]{0:T(1024)}, u32[]{:S(2)}) copy-start(f32[1024]{0:T(1024)} %param.25) | copy-start | bytes 12292
  183.2 194.3 %reduce-scatter.9.cloned.1.call-start = ((), (), s32[]{:S(2)}) async-start(), calls=%async_computation.9 | async-start | bytes 9437184 | tf_op jit(solution)/shard_map/reduce_scatter | solution.py:37
  281.1 22.8 %copy-start.29 = (bf16[2048,1024]{1,0:T(8,128)(2,1)S(1)}, bf16[2048,1024]{1,0:T(8,128)(2,1)}, u32[]{:S(2)}) copy-start(bf16[2048,1024]{1,0:T(8,128)(2,1)} %param.24) | copy-start | bytes 12582916
  315.1 127.9 %reduce-scatter.7.cloned.1.call-start = ((), (), s32[]{:S(2)}) async-start(), calls=%async_computation.7 | async-start | bytes 9437184 | tf_op jit(solution)/shard_map/reduce_scatter | solution.py:37
  330.5 112.5 %copy-start.27 = (f32[2048]{0:T(1024)S(1)}, f32[2048]{0:T(1024)}, u32[]{:S(2)}) copy-start(f32[2048]{0:T(1024)} %param.27) | copy-start | bytes 24580
  330.5 169.4 %all-gather.11.cloned.1.call-start = ((), (), s32[]{:S(2)}) async-start(), calls=%async_computation.10 | async-start | bytes 9437184 | tf_op jit(solution)/shard_map/all_gather | solution.py:33
  451.4 217.6 %reduce-scatter.11.cloned.1.call-start = ((), (), s32[]{:S(2)}) async-start(), calls=%async_computation.11 | async-start | bytes 9437184 | tf_op jit(solution)/shard_map/reduce_scatter | solution.py:37
  576.5 9.7 %copy-start.4 = (bf16[1,2048,2,1,128]{1,4,2,3,0:T(8,128)(2,1)S(1)}, bf16[1,2048,2,1,128]{1,4,2,3,0:T(8,128)(2,1)}, u32[]{:S(2)}) copy-start(bf16[1,2048,2,1,128]{1,4,2,3,0:T(8,128)(2,1)} %fusion.85) | copy-start | bytes 3145732
  576.5 9.7 %copy-start.10 = (bf16[1,2048,2,1,128]{1,4,2,3,0:T(8,128)(2,1)S(1)}, bf16[1,2048,2,1,128]{1,4,2,3,0:T(8,128)(2,1)}, u32[]{:S(2)}) copy-start(bf16[1,2048,2,1,128]{1,4,2,3,0:T(8,128)(2,1)} %fusion.82) | copy-start | bytes 3145732
  609.6 16.9 %copy-start.5 = (bf16[1,2048,2,1,128]{1,4,2,3,0:T(8,128)(2,1)S(1)}, bf16[1,2048,2,1,128]{1,4,2,3,0:T(8,128)(2,1)}, u32[]{:S(2)}) copy-start(bf16[1,2048,2,1,128]{1,4,2,3,0:T(8,128)(2,1)} %fusion.85) | copy-start | bytes 3145732
  609.6 16.9 %copy-start.7 = (bf16[1,2048,2,1,128]{1,4,2,3,0:T(8,128)(2,1)S(1)}, bf16[1,2048,2,1,128]{1,4,2,3,0:T(8,128)(2,1)}, u32[]{:S(2)}) copy-start(bf16[1,2048,2,1,128]{1,4,2,3,0:T(8,128)(2,1)} %copy-done.6) | copy-start | bytes 3145732
  609.6 16.9 %copy-start.11 = (bf16[1,2048,2,1,128]{1,4,2,3,0:T(8,128)(2,1)S(1)}, bf16[1,2048,2,1,128]{1,4,2,3,0:T(8,128)(2,1)}, u32[]{:S(2)}) copy-start(bf16[1,2048,2,1,128]{1,4,2,3,0:T(8,128)(2,1)} %fusion.82) | copy-start | bytes 3145732
  609.6 56.0 %slice-start = ((s8[8388608]{0:T(1024)(128)(4,1)}), s8[4194304]{0:T(1024)(128)(4,1)S(1)}, s32[]{:S(2)}) async-start(s8[8388608]{0:T(1024)(128)(4,1)} %bitcast.136), calls=%async_computation.12 | async-start | bytes 8388608
  626.4 39.1 %slice-start.1 = ((s8[8388608]{0:T(1024)(128)(4,1)}), s8[4194304]{0:T(1024)(128)(4,1)S(1)}, s32[]{:S(2)}) async-start(s8[8388608]{0:T(1024)(128)(4,1)} %bitcast.136), calls=%async_computation.13 | async-start | bytes 8388608
  635.8 29.7 %copy-start.9 = (bf16[2,128,2048]{2,1,0:T(8,128)(2,1)S(1)}, bf16[2,128,2048]{2,1,0:T(8,128)(2,1)}, u32[]{:S(2)}) copy-start(bf16[2,128,2048]{2,1,0:T(8,128)(2,1)} %copy-done.8) | copy-start | bytes 3145732
  (19 other events, 69.4 us)
Sparse Core Ops, SparseCore 0:
  14.5 51.1 all-gather.4
  114.4 62.2 reduce-scatter.4
  182.7 48.3 all-gather.6
  232.8 48.3 all-gather.8
  315.2 62.2 reduce-scatter.8
  380.7 62.2 reduce-scatter.6
  451.5 48.3 all-gather.10
  595.7 62.2 reduce-scatter.10
where the time goes:
time: 722 us; the launch traced here: 709 us
  waiting for transfers between devices  347 us (48%)
  matrix products  225 us (31%)
  other arithmetic  62.2 us (9%)
  local copies, waits for them, and re-layouts  35.3 us (5%)
  blocking collectives  23.5 us (3%)
  between operations  15 us (2%)
    all_gather x4, waiting for transfers between devices, seq_gather(): return lax.all_gather(values, 'tp', axis=1, tiled=True)  179 us
    reduce_scatter x4, waiting for transfers between devices, seq_reduce(): return lax.psum_scatter(values, 'tp', scatter_dimension=1, tiled=True)  168 us
    unnamed x72, local copies, waits for them, and re-layouts  35.2 us
    psum x1, blocking collectives, local_step(): grad_ln1_gamma = lax.psum(grad_ln1_gamma, 'tp')  23.5 us
    convert_element_type x1, other arithmetic, local_step(): grad_scores_bf = grad_scores.astype(jnp.bfloat16)  22.3 us
    dot_general x1, matrix products, local_step(): jnp.einsum('bsd,fd->bsf', grad_m_full, w_down, preferred_element_type=jnp...  20.8 us
    dot_general x1, matrix products, local_step(): jnp.einsum('bihe,bjhe->bhij', grad_context, v_heads, preferred_element_ty...  19.5 us
    sub x1, matrix products, local_step(): prob_f = jax.nn.softmax(jnp.where(causal, scores, MASK_VALUE), axis=-1)  19.4 us
  transfers between devices with their start and end apart: 8, of which 7 were waited for; matrix products, arithmetic and copies ran while one was open for 16% of the time, Pallas kernels for 0%

commit v1 on v0

v1 whole, which is shorter than its diff:
```python
import functools
import math
import jax
import jax.numpy as jnp
from jax import lax
from jax.experimental import pallas as pl
from jax.experimental.pallas import tpu as pltpu
from jax.sharding import PartitionSpec as P

EPS = 1e-5
MASK_VALUE = -1e30
LOG2E = math.log2(math.e)
MESH = pl.DeviceIdType.MESH
BF = jnp.bfloat16
F32 = jnp.float32
ROWS = 256
CHIP = 512
SEQ = 2048
D = 2048
TN = 512


def alibi_slopes(n_heads):
    closest = 2 ** int(math.floor(math.log2(n_heads)))
    base_ratio = 2.0 ** (-8.0 / closest)
    extra_ratio = 2.0 ** (-4.0 / closest)
    remaining = min(closest, n_heads - closest)
    slopes = [base_ratio ** (i + 1) for i in range(closest)]
    slopes = slopes + [extra_ratio ** (2 * i + 1) for i in range(remaining)]
    return jnp.array(slopes, dtype=jnp.float32)


def dot(a, b):
    return lax.dot_general(a, b, (((1,), (0,)), ((), ())), preferred_element_type=F32)


def dot_nt(a, b):
    return lax.dot_general(a, b, (((1,), (1,)), ((), ())), preferred_element_type=F32)


def dot_tn(a, b):
    return lax.dot_general(a, b, (((0,), (0,)), ((), ())), preferred_element_type=F32)


def places():
    me = lax.axis_index('tp')
    c = lax.rem(me, 2)
    delta = 1 - 2 * c
    xn = me + 2 - 4 * lax.rem(me // 2, 2)
    dy = 4 - 8 * (me // 4)
    return me, me + delta, xn, me + dy, xn + dy, delta


def entry_barrier(peers):
    sem = pltpu.get_barrier_semaphore()
    for p in peers:
        pl.semaphore_signal(sem, inc=1, device_id={'tp': p}, device_id_type=MESH)
    pl.semaphore_wait(sem, len(peers))


def rows_at(block, half=None):
    if half is None:
        return pl.ds(pl.multiple_of(block * ROWS, ROWS), ROWS)
    return pl.ds(pl.multiple_of(block * ROWS + half * 128, 128), 128)


def loop(lo, hi, fn):
    def body(i, carry):
        fn(i)
        return carry
    lax.fori_loop(lo, hi, body, 0)


class Gather:
    def __init__(self, full, ss, rs):
        self.full, self.ss, self.rs = full, ss, rs
        self.me, self.core, self.xn, self.yn, self.dg, delta = places()
        me, core, xn, yn, dg = self.me, self.core, self.xn, self.yn, self.dg
        cx, cy, cd = xn + delta, yn + delta, dg + delta
        self.send_rows = [(me, 0), (me, 1), (yn, 1), (me, 1), (me, 0), (xn, 0), (me, None),
                          (xn, 0), (xn, 1), (yn, 1), (yn, 0), (dg, 0), (dg, 1)]
        self.recv_rows = [(xn, 0), (xn, 1), (dg, 1), (yn, 1), (yn, 0), (dg, 0), (core, None),
                          (cx, 0), (cx, 1), (cy, 1), (cy, 0), (cd, 0), (cd, 1)]
        self.peer = [xn] * 3 + [yn] * 3 + [core] * 7

    def copy(self, k, rows):
        ref = self.full.at[rows_at(*rows)]
        return pltpu.make_async_remote_copy(src_ref=ref, dst_ref=ref, send_sem=self.ss.at[k], recv_sem=self.rs.at[k],
                                            device_id={'tp': self.peer[k]}, device_id_type=MESH)

    def barrier(self):
        entry_barrier([self.core, self.xn, self.yn])

    def send(self, k):
        self.copy(k, self.send_rows[k]).start()

    def recv(self, k):
        self.copy(k, self.recv_rows[k]).wait_recv()

    def run(self, compute, pre=None, landed=None):
        def chip(block):
            return pl.multiple_of((block // 2) * CHIP, CHIP)
        for k in (0, 3, 1, 4, 6):
            self.send(k)
        if pre is not None:
            pre()
        self.recv(6)
        compute(0, chip(self.me))
        self.recv(0)
        self.send(5)
        self.send(7)
        self.recv(3)
        self.send(2)
        self.send(9)
        self.recv(1)
        self.send(8)
        self.recv(4)
        self.send(10)
        self.recv(7)
        self.recv(8)
        compute(1, chip(self.xn))
        self.recv(9)
        self.recv(10)
        compute(2, chip(self.yn))
        self.recv(5)
        self.send(11)
        self.recv(2)
        self.send(12)
        if landed is not None:
            landed()
        self.recv(11)
        self.recv(12)
        compute(3, chip(self.dg))
        for k in range(13):
            self.copy(k, self.send_rows[k]).wait_send()


GATHER_SCRATCH = [pltpu.VMEM((SEQ, D), BF), pltpu.SemaphoreType.DMA((13,)), pltpu.SemaphoreType.DMA((13,))]


class Scatter:
    def __init__(self, pb, din, rel, fin, ss, rs):
        self.pb, self.din, self.rel, self.fin, self.ss, self.rs = pb, din, rel, fin, ss, rs
        self.me, self.core, self.xn, self.yn, dg, self.delta = places()
        self.block = [dg, self.xn, self.yn, self.me]

    def barrier(self):
        entry_barrier([self.core, self.xn, self.yn])

    def copy(self, k):
        lo, hi = pl.ds(0, 128), pl.ds(128, 128)
        din, rel, fin, xn, yn = self.din, self.rel, self.fin, self.xn, self.yn
        if not isinstance(k, int) or k < 4:
            src, dst, peer = self.pb.at[k], din.at[k], self.core
        else:
            src, dst, peer = ((din.at[0, lo], rel.at[0], xn), (din.at[1, lo], fin.at[0, lo], xn), (din.at[1, hi], fin.at[0, hi], xn),
                              (din.at[0, hi], rel.at[1], yn), (din.at[2, hi], fin.at[1, hi], yn), (din.at[2, lo], fin.at[1, lo], yn))[k - 4]
        return pltpu.make_async_remote_copy(src_ref=src, dst_ref=dst, send_sem=self.ss.at[k], recv_sem=self.rs.at[k],
                                            device_id={'tp': peer}, device_id_type=MESH)

    def give(self, d, tile, block=None):
        block = self.block[d] + self.delta if block is None else block
        def body(n):
            cols = pl.ds(pl.multiple_of(n * TN, TN), TN)
            self.pb[d, :, cols] = tile(block, n).astype(BF)
        loop(0, D // TN, body)
        self.copy(d).start()

    def keep(self, d, tile):
        self.copy(d).wait_recv()
        def body(n):
            cols = pl.ds(pl.multiple_of(n * TN, TN), TN)
            self.din[d, :, cols] = (tile(self.block[d], n) + self.din[d, :, cols].astype(F32)).astype(BF)
        loop(0, D // TN, body)

    def start(self, *flows):
        for k in flows:
            self.copy(k).start()

    def add_relay(self, d, half, slot):
        def body(n):
            rows = pl.ds(pl.multiple_of(half * 128 + n * 16, 16), 16)
            src = pl.ds(pl.multiple_of(n * 16, 16), 16)
            self.din[d, rows] = (self.din[d, rows].astype(F32) + self.rel[slot, src].astype(F32)).astype(BF)
        loop(0, 8, body)

    def relays(self):
        self.copy(4).wait_recv()
        self.add_relay(2, 0, 0)
        self.start(9)
        self.copy(7).wait_recv()
        self.add_relay(1, 1, 1)
        self.start(6)

    def arrive(self):
        for k in (5, 8, 6, 9):
            self.copy(k).wait_recv()

    def run(self, tile):
        self.give(0, tile)
        self.give(1, tile)
        self.keep(0, tile)
        self.start(4, 7)
        self.give(2, tile)
        self.keep(1, tile)
        self.start(5)
        self.give(3, tile)
        self.keep(2, tile)
        self.start(8)
        self.keep(3, tile)

    def total(self, rows):
        s = self.din[3, rows].astype(F32) + self.fin[0, rows].astype(F32) + self.fin[1, rows].astype(F32)
        return s.astype(BF).astype(F32)

    def finish(self, first=0):
        for k in range(first, 10):
            self.copy(k).wait_send()


SCATTER_REST = [pltpu.VMEM((4, ROWS, D), BF), pltpu.VMEM((2, 128, D), BF), pltpu.VMEM((2, ROWS, D), BF),
                pltpu.SemaphoreType.DMA((10,)), pltpu.SemaphoreType.DMA((10,))]
SCATTER_SCRATCH = [pltpu.VMEM((4, ROWS, D), BF)] + SCATTER_REST
VM = pl.BlockSpec(memory_space=pltpu.VMEM)
HB = pl.BlockSpec(memory_space=pl.ANY)


def call(body, name, cid, ins, outs, scratch, args, flops):
    return pl.pallas_call(
        body,
        name=name,
        out_shape=[jax.ShapeDtypeStruct(s, t) for s, t, _ in outs],
        in_specs=ins,
        out_specs=[m for _, _, m in outs],
        scratch_shapes=scratch,
        compiler_params=pltpu.CompilerParams(collective_id=cid, has_side_effects=True, vmem_limit_bytes=67043328),
        cost_estimate=pl.CostEstimate(flops=flops, bytes_accessed=32 << 20, transcendentals=0),
    )(*args)


def norm_rows(v, gain, bias):
    mean = jnp.mean(v, axis=-1, keepdims=True)
    cent = v - mean
    var = jnp.mean(cent * cent, axis=-1, keepdims=True)
    return cent * lax.rsqrt(var + EPS) * gain + bias


def norm_rows_back(v, gain, ct):
    mean = jnp.mean(v, axis=-1, keepdims=True)
    cent = v - mean
    rstd = lax.rsqrt(jnp.mean(cent * cent, axis=-1, keepdims=True) + EPS)
    xhat = cent * rstd
    gx = ct * gain
    m1 = jnp.mean(gx, axis=-1, keepdims=True)
    m2 = jnp.mean(gx * xhat, axis=-1, keepdims=True)
    return rstd * (gx - m1 - xhat * m2), xhat


RB = 32


def row_blocks(fn):
    loop(0, ROWS // RB, lambda i: fn(pl.ds(pl.multiple_of(i * RB, RB), RB)))


def front_kernel(sl_ref, x_hbm, g1_ref, b1_ref, w6_hbm, bq_ref, gyl_hbm, wo_hbm, bo_ref, g2_ref, b2_ref,
                 qkv_out, ctx_out, lse_ref, h_out, gy_out, x1_ref, gl_ref,
                 full, ss, rs, gyf, ssy, rsy, x, w6, wo, qkv, ctx, bias, biasm, acc, ml, ls, hs, ys, *scratch):
    ag = Gather(full, ss, rs)
    gg = Gather(gyf, ssy, rsy)
    sc = Scatter(*scratch)
    pairs = [(x_hbm, x), (gyl_hbm, gyf.at[rows_at(ag.me)]), (w6_hbm, w6), (wo_hbm, wo)]
    loads = [pltpu.make_async_copy(src, dst, ls.at[i]) for i, (src, dst) in enumerate(pairs)]
    for l in loads:
        l.start()
    loads[0].wait()

    def ln(i):
        rows = pl.ds(pl.multiple_of(i * RB, RB), RB)
        dst = pl.ds(pl.multiple_of(ag.me * ROWS + i * RB, RB), RB)
        full[dst] = norm_rows(x[rows].astype(F32), g1_ref[...], b1_ref[...]).astype(BF)
    loop(0, ROWS // RB, ln)
    ag.barrier()
    c1 = (128 ** -0.5) * LOG2E

    def biases():
        ki = lax.broadcasted_iota(jnp.int32, (CHIP, CHIP), 0)
        qi = lax.broadcasted_iota(jnp.int32, (CHIP, CHIP), 1)
        for h in range(2):
            b = ki.astype(F32) * (sl_ref[h] * LOG2E)
            bias[h] = b
            biasm[h] = jnp.where(ki <= qi, b, MASK_VALUE)
        for l in loads[1:]:
            l.wait()

    def compute(idx, r0):
        rows = pl.ds(r0, CHIP)
        pltpu.make_async_copy(full.at[rows], h_out.at[rows], hs.at[idx]).start()
        def body(t):
            cols = pl.ds(pl.multiple_of(t * 256, 256), 256)
            w = jnp.concatenate([w6[2 * t], w6[2 * t + 1]], axis=1)
            qkv[rows, cols] = (dot(full[rows], w) + bq_ref[:, cols]).astype(BF)
        loop(0, 3, body)

    def start_gy():
        for k in (0, 3, 1, 4, 6):
            gg.send(k)
    ag.run(compute, pre=biases, landed=start_gy)
    stores = [pltpu.make_async_copy(qkv, qkv_out, ls.at[4]), pltpu.make_async_copy(ctx, ctx_out, ls.at[5])]
    stores[0].start()

    def tile(block, n):
        cols = pl.ds(pl.multiple_of(n * TN, TN), TN)
        return dot(ctx[rows_at(block)], wo[:, cols])

    xb = lax.rem(ag.me // 2, 2)
    yb = ag.me // 4

    def attend(p):
        nx = xb + (1 - p // 2) * (1 - 2 * xb)
        ny = yb + (1 - lax.rem(p, 2)) * (1 - 2 * yb)
        i = 2 * ny + nx
        qrows = pl.ds(pl.multiple_of(i * CHIP, CHIP), CHIP)

        def one(h):
            lanes = [pl.ds(pl.multiple_of((2 * t + h) * 128, 128), 128) for t in range(3)]
            sl = sl_ref[h] * LOG2E
            q = qkv[qrows, lanes[0]]
            ml[0:1] = jnp.full((1, CHIP), MASK_VALUE, F32)
            ml[1:2] = jnp.zeros((1, CHIP), F32)
            acc[...] = jnp.zeros_like(acc)
            def step(j, bias_ref):
                krows = pl.ds(pl.multiple_of(j * CHIP, CHIP), CHIP)
                s = dot_nt(qkv[krows, lanes[1]], q) * c1 + bias_ref[h]
                cj = sl * (j * CHIP).astype(F32)
                m = ml[0:1]
                mn = jnp.maximum(m, jnp.max(s, axis=0, keepdims=True) + cj)
                pr = jnp.exp2(s - (mn - cj))
                alpha = jnp.exp2(m - mn)
                ml[1:2] = ml[1:2] * alpha + jnp.sum(pr, axis=0, keepdims=True)
                ml[0:1] = mn
                acc[...] = acc[...] * alpha + dot_tn(qkv[krows, lanes[2]], pr.astype(BF))
            loop(0, i, lambda j: step(j, bias))
            step(i, biasm)
            ctx[qrows, lanes[0]] = jnp.transpose(acc[...] / ml[1:2]).astype(BF)
            lse_ref[h, :, qrows] = ml[0:1] + jnp.log(ml[1:2]) * LOG2E
        loop(0, 2, one)
        sc.give(p, tile, 2 * i + 1 - lax.rem(ag.me, 2))
    loop(0, 4, attend)
    stores[1].start()

    gg.recv(0)
    gg.send(5)
    gg.send(7)
    gg.recv(3)
    gg.send(2)
    gg.send(9)
    sc.keep(0, tile)
    sc.start(4, 7)
    sc.keep(1, tile)
    sc.start(5)
    sc.keep(2, tile)
    sc.start(8)
    sc.keep(3, tile)
    gg.recv(1)
    gg.send(8)
    gg.recv(4)
    gg.send(10)

    chips = [pl.multiple_of((b // 2) * CHIP, CHIP) for b in (ag.me, ag.xn, ag.yn, ag.dg)]
    def keep_gy(i):
        rows = pl.ds(chips[i], CHIP)
        return pltpu.make_async_copy(gyf.at[rows], gy_out.at[rows], ys.at[i])
    gg.recv(6)
    keep_gy(0).start()
    sc.relays()
    for k in (7, 8):
        gg.recv(k)
    keep_gy(1).start()
    for k in (9, 10):
        gg.recv(k)
    keep_gy(2).start()
    gg.recv(5)
    gg.send(11)
    gg.recv(2)
    gg.send(12)
    sc.arrive()

    def fin(rows):
        x1 = x[rows].astype(F32) + sc.total(rows) + bo_ref[...]
        x1_ref[rows] = x1
        gl_ref[rows] = norm_rows(x1, g2_ref[...], b2_ref[...]).astype(BF)
    row_blocks(fin)
    for k in (11, 12):
        gg.recv(k)
    keep_gy(3).start()
    sc.finish()
    for k in range(13):
        gg.copy(k, gg.send_rows[k]).wait_send()
    for s in stores:
        s.wait()
    for i in range(4):
        rows = pl.ds(i * CHIP, CHIP)
        pltpu.make_async_copy(full.at[rows], h_out.at[rows], hs.at[i]).wait()
        keep_gy(i).wait()


def mlp_kernel(g_hbm, gy_hbm, wu_hbm, bu_ref, wd_hbm, x1_hbm, g2_ref,
               r_out, gm_ref, gmb_ref, vec_ref, gwu_out, gwd_out, gbu_ref, gbd_ref,
               full, ss, rs, gy, wu, wd, x1, gp, r, gw, ls, ys, *scratch):
    ag = Gather(full, ss, rs)
    sc = Scatter(*scratch)
    own = pltpu.make_async_copy(g_hbm, full.at[rows_at(ag.me)], ls.at[0])
    own.start()
    load_wd = pltpu.make_async_copy(wd_hbm, wd, ls.at[1])
    load_wd.start()
    chips = [pl.multiple_of((b // 2) * CHIP, CHIP) for b in (ag.me, ag.xn, ag.yn, ag.dg)]
    load_gy = [pltpu.make_async_copy(gy_hbm.at[pl.ds(c, CHIP)], gy.at[pl.ds(c, CHIP)], ys.at[i]) for i, c in enumerate(chips)]
    for l in load_gy:
        l.start()
    load_wu = pltpu.make_async_copy(wu_hbm, wu, ls.at[2])
    load_wu.start()
    load_x1 = pltpu.make_async_copy(x1_hbm, x1, ls.at[3])
    load_x1.start()
    own.wait()
    ag.barrier()
    for k in (0, 3, 1, 4, 6):
        ag.send(k)
    gbu_ref[...] = jnp.zeros_like(gbu_ref)
    gbd_ref[...] = jnp.zeros_like(gbd_ref)
    vec_ref[...] = jnp.zeros_like(vec_ref)

    def act(i):
        rows = pl.ds(chips[i], CHIP)
        load_gy[i].wait()
        def body(n):
            cols = pl.ds(pl.multiple_of(n * 256, 256), 256)
            gp[rows, cols] = dot_nt(gy[rows], wd[cols]).astype(BF)
        loop(0, 4, body)

    def colsum(n):
        part = pl.ds(pl.multiple_of(n * RB, RB), RB)
        gbd_ref[...] += jnp.sum(gy[part].astype(F32), axis=0, keepdims=True)

    k0 = math.sqrt(2.0 / math.pi)
    k1 = 0.044715

    def up(i):
        rows = pl.ds(chips[i], CHIP)
        def body(n):
            cols = pl.ds(pl.multiple_of(n * 256, 256), 256)
            z = dot(full[rows], wu[:, cols]) + bu_ref[:, cols]
            z2 = z * z
            t = jnp.tanh(k0 * (z + k1 * (z2 * z)))
            half = 0.5 * (1.0 + t)
            r[rows, cols] = (z * half).astype(BF)
            dz = half + (0.5 * z) * (1.0 - t * t) * (k0 * (1.0 + 3.0 * k1 * z2))
            gpre = gp[rows, cols].astype(F32) * dz
            gbu_ref[:, cols] += jnp.sum(gpre, axis=0, keepdims=True)
            gp[rows, cols] = gpre.astype(BF)
        loop(0, 4, body)
        pltpu.make_async_copy(r.at[rows], r_out.at[rows], ys.at[i]).start()

    def tile(block, n):
        cols = pl.ds(pl.multiple_of(n * TN, TN), TN)
        return dot_nt(gp[rows_at(block)], wu[cols])

    load_wd.wait()
    act(0)
    load_wu.wait()
    ag.recv(6)
    up(0)
    act(1)
    ag.recv(0)
    ag.send(5)
    ag.send(7)
    ag.recv(3)
    ag.send(2)
    ag.send(9)
    act(2)
    act(3)
    loop(0, SEQ // RB // 2, colsum)
    ag.recv(1)
    ag.send(8)
    ag.recv(4)
    ag.send(10)
    ag.recv(7)
    ag.recv(8)
    up(1)
    sc.give(1, tile)
    ag.recv(9)
    ag.recv(10)
    up(2)
    sc.give(2, tile)
    ag.recv(5)
    ag.send(11)
    ag.recv(2)
    ag.send(12)
    sc.keep(1, tile)
    sc.start(5)
    sc.keep(2, tile)
    sc.start(8)
    ag.recv(11)
    ag.recv(12)
    up(3)
    sc.give(0, tile)
    sc.give(3, tile)
    sc.keep(0, tile)
    sc.start(4, 7)
    sc.keep(3, tile)

    def gwu_step(i):
        cols = pl.ds(pl.multiple_of(i * 256, 256), 256)
        gw[:, pl.ds(0, 1024)] = dot_tn(full[:, cols], gp[...]).astype(BF)
        c = pltpu.make_async_copy(gw.at[:, pl.ds(0, 1024)], gwu_out.at[cols], ls.at[4])
        c.start()
        c.wait()

    def gwd_step(i):
        cols = pl.ds(pl.multiple_of(i * 256, 256), 256)
        gw[...] = dot_tn(r[:, cols], gy[...]).astype(BF)
        c = pltpu.make_async_copy(gw, gwd_out.at[cols], ls.at[4])
        c.start()
        c.wait()

    loop(0, 6, gwu_step)
    sc.relays()
    loop(6, 8, gwu_step)
    loop(0, 4, gwd_step)
    loop(SEQ // RB // 2, SEQ // RB, colsum)
    load_x1.wait()
    sc.arrive()

    def fin(rows):
        ct = sc.total(rows)
        dx, xhat = norm_rows_back(x1[rows], g2_ref[...], ct)
        mine = pl.ds(pl.multiple_of(ag.me * ROWS + rows.start, RB), RB)
        gm = gy[mine].astype(F32) + dx
        gm_ref[rows] = gm
        gmb_ref[rows] = gm.astype(BF)
        vec_ref[0:1] += jnp.sum(ct * xhat, axis=0, keepdims=True)
        vec_ref[1:2] += jnp.sum(ct, axis=0, keepdims=True)
        vec_ref[2:3] += jnp.sum(gm, axis=0, keepdims=True)
    row_blocks(fin)
    for k in range(13):
        ag.copy(k, ag.send_rows[k]).wait_send()
    sc.finish()
    for i in range(4):
        rows = pl.ds(chips[i], CHIP)
        pltpu.make_async_copy(r.at[rows], r_out.at[rows], ys.at[i]).wait()


def tail_kernel(sl_ref, gm_hbm, wo_hbm, r_hbm, wd_hbm, qkv_hbm, ctx_hbm, lse_ref, w6_hbm, x_hbm, gmf_hbm, x1_hbm, bd_ref, g1_ref,
                h_hbm, vec2_ref, y_ref, gx_ref, vec_out, gwq_out, gwo_out, gb_ref,
                full, ss, rs, wo, r, wd, qkv, ctx, w6, x1, gc, gq, gwq, gwo, bias, biasm, delta, dqt, dk, dv, vec, bufv,
                ls, vs, vr, pb, din1, rel1, fin1, ss1, rs1, din2, rel2, fin2, ss2, rs2):
    ag = Gather(full, ss, rs)
    s1 = Scatter(pb, din1, rel1, fin1, ss1, rs1)
    s2 = Scatter(pb, din2, rel2, fin2, ss2, rs2)
    pairs = [(gm_hbm, full.at[rows_at(ag.me)]), (wd_hbm, wd), (r_hbm, r), (wo_hbm, wo), (qkv_hbm, qkv), (ctx_hbm, ctx), (w6_hbm, w6),
             (x1_hbm, x1)]
    loads = [pltpu.make_async_copy(src, dst, ls.at[i]) for i, (src, dst) in enumerate(pairs)]
    for l in loads:
        l.start()
    loads[0].wait()
    peers = [lax.rem(ag.me + k, 8) for k in range(1, 8)]
    entry_barrier(peers)
    for k in (0, 3, 1, 4, 6):
        ag.send(k)
    scale = 128 ** -0.5
    c1 = scale * LOG2E
    vec[...] = vec2_ref[...]
    gb_ref[...] = jnp.zeros_like(gb_ref)

    def mtile(block, n):
        cols = pl.ds(pl.multiple_of(n * TN, TN), TN)
        return dot(r[rows_at(block)], wd[:, cols])

    def gcs(block):
        rows = pl.ds(pl.multiple_of((block // 2) * CHIP, CHIP), CHIP)
        gc[rows] = dot_nt(full[rows], wo[...]).astype(BF)

    loads[1].wait()
    loads[2].wait()
    for d in range(4):
        s1.give(d, mtile)
    s1.keep(0, mtile)
    loads[3].wait()
    ag.recv(6)
    gcs(ag.me)
    ag.recv(0)
    ag.send(5)
    ag.send(7)
    ag.recv(3)
    ag.send(2)
    ag.send(9)
    for d in range(1, 4):
        s1.keep(d, mtile)
    load_h = [pltpu.make_async_copy(h_hbm.at[:, pl.ds(i * 1024, 1024)], r, ls.at[10 + i]) for i in range(2)]
    load_h[0].start()
    for l in loads[4:]:
        l.wait()

    def rowsum(i):
        rows = pl.ds(pl.multiple_of(i * CHIP, CHIP), CHIP)
        for h in range(2):
            lanes = pl.ds(h * 128, 128)
            prod = gc[rows, lanes].astype(F32) * ctx[rows, lanes].astype(F32)
            delta[h:h + 1, rows] = jnp.sum(jnp.transpose(prod), axis=0, keepdims=True)

    ag.recv(1)
    ag.send(8)
    ag.recv(4)
    ag.send(10)
    ag.recv(7)
    ag.recv(8)
    gcs(ag.xn)
    ag.recv(9)
    ag.recv(10)
    gcs(ag.yn)
    ag.recv(5)
    ag.send(11)
    ag.recv(2)
    ag.send(12)
    s1.start(4, 7, 5, 8)
    ag.recv(11)
    ag.recv(12)
    gcs(ag.dg)
    x = wo
    load_x = pltpu.make_async_copy(x_hbm, x, ls.at[8])
    load_x.start()
    loop(0, SEQ // CHIP, rowsum)

    def put(h, t, rows, val):
        val = val.astype(BF)
        gq[rows, (2 * t + h) * 128:(2 * t + h + 1) * 128] = val
        gb_ref[h, t:t + 1] += jnp.sum(val.astype(F32), axis=0, keepdims=True)

    def head(h):
        sl = sl_ref[h] * LOG2E
        ki = lax.broadcasted_iota(jnp.int32, (CHIP, CHIP), 0)
        qi = lax.broadcasted_iota(jnp.int32, (CHIP, CHIP), 1)
        b = ki.astype(F32) * sl
        bias[...] = b
        biasm[...] = jnp.where(ki <= qi, b, MASK_VALUE)
        dqt[...] = jnp.zeros_like(dqt)
        lq, lk, lv, lo = (pl.ds((2 * t + h) * 128, 128) for t in (0, 1, 2, 0))

        def kblock(j):
            krows = pl.ds(pl.multiple_of(j * CHIP, CHIP), CHIP)
            k = qkv[krows, lk]
            v = qkv[krows, lv]
            dk[...] = jnp.zeros_like(dk)
            dv[...] = jnp.zeros_like(dv)
            cj = sl * (j * CHIP).astype(F32)
            def step(i, bias_ref):
                qrows = pl.ds(pl.multiple_of(i * CHIP, CHIP), CHIP)
                q = qkv[qrows, lq]
                do = gc[qrows, lo]
                p = jnp.exp2(dot_nt(k, q) * c1 + bias_ref[...] - (lse_ref[h, :, qrows] - cj))
                dv[...] += dot(p.astype(BF), do)
                ds = (p * (dot_nt(v, do) - delta[h:h + 1, qrows])).astype(BF)
                dk[...] += dot(ds, q)
                dqt[:, qrows] += dot_tn(k, ds)
            step(j, biasm)
            loop(j + 1, SEQ // CHIP, lambda i: step(i, bias))
            put(h, 1, krows, dk[...] * scale)
            put(h, 2, krows, dv[...])
        loop(0, SEQ // CHIP, kblock)

        def qout(i):
            rows = pl.ds(pl.multiple_of(i * CHIP, CHIP), CHIP)
            put(h, 0, rows, jnp.transpose(dqt[:, rows]) * scale)
        loop(0, SEQ // CHIP, qout)

    head(0)
    s1.relays()
    head(1)

    def htile(block, n):
        rows = rows_at(block)
        cols = pl.ds(pl.multiple_of(n * TN, TN), TN)
        out = None
        for t in range(3):
            w = jnp.concatenate([w6[2 * t, cols], w6[2 * t + 1, cols]], axis=1)
            part = dot_nt(gq[rows, t * 256:(t + 1) * 256], w)
            out = part if out is None else out + part
        return out

    for k in range(4):
        s1.copy(k).wait_send()
    s2.run(htile)

    stores = [pltpu.make_async_copy(gwq, gwq_out.at[pl.ds(i * 1024, 1024)], ls.at[12]) for i in range(2)]
    stores.append(pltpu.make_async_copy(gwo, gwo_out, ls.at[13]))

    def wq():
        def body(i):
            src = pl.ds(pl.multiple_of(i * 256, 256), 256)
            gwq[src] = dot_tn(r[:, src], gq[...]).astype(BF)
        return body

    load_h[0].wait()
    loop(0, 4, wq())
    load_h[1].start()
    stores[0].start()
    s2.relays()
    s1.arrive()

    def yrow(rows):
        y_ref[rows] = (x1[rows] + s1.total(rows) + bd_ref[...]).astype(BF)
    row_blocks(yrow)
    gm = x1
    load_gm = pltpu.make_async_copy(gmf_hbm, gm, ls.at[9])
    load_gm.start()

    def wout(n):
        cols = pl.ds(pl.multiple_of(n * TN, TN), TN)
        gwo[:, cols] = dot_tn(ctx[...], full[:, cols]).astype(BF)
    loop(0, D // TN, wout)
    stores[2].start()
    load_h[1].wait()
    stores[0].wait()
    loop(0, 4, wq())
    stores[1].start()
    load_x.wait()
    load_gm.wait()
    s2.arrive()

    def fin(rows):
        ct = s2.total(rows)
        dx, xhat = norm_rows_back(x[rows].astype(F32), g1_ref[...], ct)
        gx_ref[rows] = (gm[rows] + dx).astype(BF)
        vec[3:4] += jnp.sum(ct * xhat, axis=0, keepdims=True)
        vec[4:5] += jnp.sum(ct, axis=0, keepdims=True)
    row_blocks(fin)
    s1.finish(4)
    s2.finish()
    copies = [pltpu.make_async_remote_copy(src_ref=vec, dst_ref=bufv.at[ag.me], send_sem=vs.at[k], recv_sem=vr.at[k],
                                           device_id={'tp': peers[k]}, device_id_type=MESH) for k in range(7)]
    for c in copies:
        c.start()
    bufv[ag.me] = vec[...]
    for k in range(13):
        ag.copy(k, ag.send_rows[k]).wait_send()
    for s in stores[1:]:
        s.wait()
    for c in copies:
        c.wait()
    total = bufv[0]
    for i in range(1, 8):
        total = total + bufv[i]
    vec_out[...] = total


def solution(mesh):
    def local_step(x, ln1_gamma, ln1_beta, w_qkv, b_qkv, w_out, b_out, ln2_gamma, ln2_beta, w_up, b_up, w_down, b_down, grad_y):
        tp_index = lax.axis_index('tp')
        slopes = lax.dynamic_slice_in_dim(alibi_slopes(16), tp_index * 2, 2)
        row = lambda v: v.reshape(1, -1)
        x2, gy2 = x[0], grad_y[0]
        w6 = w_qkv.transpose(2, 1, 0, 3).reshape(6, D, 128)
        bq = b_qkv.transpose(1, 0, 2).reshape(1, 768)

        qkv, ctx, lse, h_full, gy_full, x1, g_loc = call(
            front_kernel, 'front', 0, [pl.BlockSpec(memory_space=pltpu.SMEM), HB, VM, VM, HB, VM, HB, HB, VM, VM, VM],
            [((SEQ, 768), BF, HB), ((SEQ, 256), BF, HB), ((2, 1, SEQ), F32, VM), ((SEQ, D), BF, HB), ((SEQ, D), BF, HB),
             ((ROWS, D), F32, VM), ((ROWS, D), BF, VM)],
            GATHER_SCRATCH * 2 + [pltpu.VMEM((ROWS, D), BF), pltpu.VMEM((6, D, 128), BF), pltpu.VMEM((256, D), BF),
                                  pltpu.VMEM((SEQ, 768), BF), pltpu.VMEM((SEQ, 256), BF), pltpu.VMEM((2, CHIP, CHIP), F32),
                                  pltpu.VMEM((2, CHIP, CHIP), F32), pltpu.VMEM((128, CHIP), F32), pltpu.VMEM((8, CHIP), F32),
                                  pltpu.SemaphoreType.DMA((6,)), pltpu.SemaphoreType.DMA((4,)), pltpu.SemaphoreType.DMA((4,))]
            + SCATTER_SCRATCH,
            (slopes, x2, row(ln1_gamma), row(ln1_beta), w6, bq, gy2, w_out, row(b_out), row(ln2_gamma), row(ln2_beta)), 12 << 30)
        r, gm, gm_bf, vec2, g_wu, g_wd, gbu, gbd = call(
            mlp_kernel, 'mlp', 2, [HB, HB, HB, VM, HB, HB, VM],
            [((SEQ, 1024), BF, HB), ((ROWS, D), F32, VM), ((ROWS, D), BF, VM), ((8, D), F32, VM), ((D, 1024), BF, HB),
             ((1024, D), BF, HB), ((1, 1024), F32, VM), ((1, D), F32, VM)],
            GATHER_SCRATCH + [pltpu.VMEM((SEQ, D), BF), pltpu.VMEM((D, 1024), BF), pltpu.VMEM((1024, D), BF), pltpu.VMEM((ROWS, D), F32),
                              pltpu.VMEM((SEQ, 1024), BF), pltpu.VMEM((SEQ, 1024), BF), pltpu.VMEM((256, D), BF),
                              pltpu.SemaphoreType.DMA((5,)), pltpu.SemaphoreType.DMA((4,))] + SCATTER_SCRATCH,
            (g_loc, gy_full, w_up, row(b_up), w_down, x1, row(ln2_gamma)), 45 << 30)
        y, g_x, vec, g_wq, g_wo, g_bq = call(
            tail_kernel, 'tail', 3, [pl.BlockSpec(memory_space=pltpu.SMEM)] + [HB] * 6 + [VM] + [HB] * 4 + [VM] * 2 + [HB, VM],
            [((ROWS, D), BF, VM), ((ROWS, D), BF, VM), ((8, D), F32, VM), ((D, 768), BF, HB), ((256, D), BF, HB), ((2, 3, 128), F32, VM)],
            GATHER_SCRATCH + [pltpu.VMEM((256, D), BF), pltpu.VMEM((SEQ, 1024), BF), pltpu.VMEM((1024, D), BF), pltpu.VMEM((SEQ, 768), BF),
                              pltpu.VMEM((SEQ, 256), BF), pltpu.VMEM((6, D, 128), BF), pltpu.VMEM((ROWS, D), F32),
                              pltpu.VMEM((SEQ, 256), BF), pltpu.VMEM((SEQ, 768), BF), pltpu.VMEM((1024, 768), BF),
                              pltpu.VMEM((256, D), BF), pltpu.VMEM((CHIP, CHIP), F32), pltpu.VMEM((CHIP, CHIP), F32),
                              pltpu.VMEM((2, SEQ), F32), pltpu.VMEM((128, SEQ), F32), pltpu.VMEM((CHIP, 128), F32),
                              pltpu.VMEM((CHIP, 128), F32), pltpu.VMEM((8, D), F32), pltpu.VMEM((8, 8, D), F32),
                              pltpu.SemaphoreType.DMA((14,)), pltpu.SemaphoreType.DMA((7,)), pltpu.SemaphoreType.DMA((7,))]
            + SCATTER_SCRATCH + SCATTER_REST,
            (slopes, gm_bf, w_out, r, w_down, qkv, ctx, lse, w6, x2, gm, x1, row(b_down), row(ln1_gamma), h_full, vec2), 55 << 30)
        g_wq = g_wq.reshape(D, 3, 2, 128).transpose(0, 2, 1, 3)
        return (y[None], g_x[None], vec[3], vec[4], g_wq, g_bq, g_wo, vec[2], vec[0], vec[1], g_wu, gbu[0], g_wd, gbd[0])

    row_spec = P('dp', 'tp', None)
    in_specs = (row_spec, P(), P(), P(None, 'tp', None, None), P('tp', None, None), P('tp', None), P(), P(), P(),
                P(None, 'tp'), P('tp'), P('tp', None), P(), row_spec)
    out_specs = (row_spec, row_spec, P('dp'), P('dp'), P('dp', 'tp', None, None), P(('dp', 'tp'), None, None),
                 P(('dp', 'tp'), None), P('dp'), P('dp'), P('dp'), P('dp', 'tp'), P(('dp', 'tp')), P(('dp', 'tp'), None), P('dp'))
    return jax.shard_map(local_step, mesh=mesh, in_specs=in_specs, out_specs=out_specs, check_vma=False)
```

time: 722 us -> 358 us (0.50); the launches traced: 709 us -> 357 us
  waiting for transfers between devices: 347 us -> 0 us
  Pallas kernels: 0 us -> 332 us
  matrix products: 225 us -> 0 us
  other arithmetic: 62.2 us -> 0 us
  blocking collectives: 23.5 us -> 0 us
  between operations: 15 us -> 0.69 us
  local copies, waits for them, and re-layouts: 35.3 us -> 24.6 us
    pallas_call x0 -> x3, Pallas kernels: none -> 332 us  [call(): pl.pallas_call(body, name=name, out_shape=[jax.ShapeDtypeStruct(s, t) for...]
    dot_general x17 -> x0, matrix products: 206 us -> none  [the longest x1 20.8 us: local_step(): jnp.einsum('bsd,fd->bsf', grad_m_full, w_down, preferred_element_type=jnp...]
    all_gather x4 -> x0, waiting for transfers between devices: 179 us -> none  [seq_gather(): return lax.all_gather(values, 'tp', axis=1, tiled=True)]
    reduce_scatter x4 -> x0, waiting for transfers between devices: 168 us -> none  [seq_reduce(): return lax.psum_scatter(values, 'tp', scatter_dimension=1, tiled=True)]
    convert_element_type x6 -> x0, other arithmetic: 31.7 us -> none  [the longest x1 22.3 us: local_step(): grad_scores_bf = grad_scores.astype(jnp.bfloat16)]
    reduce_sum x10 -> x0, other arithmetic: 26.2 us -> none  [the longest x4 11.8 us: layer_norm(): return centered * lax.rsqrt(variance + EPS) * ln_gain + ln_bias]
    unnamed x72 -> x22, local copies, waits for them, and re-layouts: 35.2 us -> 10.7 us
    psum x1 -> x0, blocking collectives: 23.5 us -> none  [local_step(): grad_ln1_gamma = lax.psum(grad_ln1_gamma, 'tp')]
  transfers between devices with their start and end apart: 8 -> 0, of which waited for: 7 -> 0; matrix products, arithmetic and copies ran while one was open for 16% -> 0% of each run, Pallas kernels for 0% -> 0%
where the time goes in v1:
time: 358 us; the launch traced here: 357 us
  Pallas kernels  332 us (93%)
  local copies, waits for them, and re-layouts  24.6 us (7%)
    pallas_call x3, Pallas kernels, call(): pl.pallas_call(body, name=name, out_shape=[jax.ShapeDtypeStruct(s, t) for...  332 us
    unnamed x22, local copies, waits for them, and re-layouts  10.7 us

profile of v1, /device:TPU:0, one launch (start us, length us, event | category | flops | bytes accessed | tf_op | source)
XLA Modules:
  0.0 357.2 jit_solution(17420857973304902616)
XLA Ops:
  0.6 1.2 dynamic_slice.3.sl_ref
  1.9 4.0 %copy.29 = bf16[3,2,2048,128]{3,2,1,0:T(8,128)(2,1)} copy(bf16[3,2,2048,128]{3,1,0,2:T(2,128)(2,1)} %bitcast.24) | data formatting | bytes 6291456 | tf_op jit(solution)/shard_map/transpose | solution.py:762
  5.9 117.5 %front.1 = (bf16[2048,768]{1,0:T(8,128)(2,1)}, bf16[2048,256]{1,0:T(8,128)(2,1)}, f32[2,1,2048]{2,1,0:T(1,128)}, bf16[2048,2048]{1,0:T(8,128)(2,1)}, bf16[2048,2...) custom-call(f32[2]{0:T(128)} %dynamic_slice.3.sl_ref, bf16[256,2048]{1,0:T(8,128)(2,1)} %bitcast.38, ...), custom_call_target="tpu_custom_call" | custom-call | flops 12884901888 | bytes 33554432 | tf_op jit(solution)/shard_map/front/pallas_call | solution.py:229
  123.3 95.3 %mlp.1 = (bf16[2048,1024]{1,0:T(8,128)(2,1)}, f32[256,2048]{1,0:T(8,128)}, bf16[256,2048]{1,0:T(8,128)(2,1)}, f32[8,2048]{1,0:T(8,128)}, bf16[2048,1024]{1,0:T(8...) custom-call(bf16[256,2048]{1,0:T(8,128)(2,1)} %get-tuple-element.35.g_hbm, ...), custom_call_target="tpu_custom_call" | custom-call | flops 48318382080 | bytes 33554432 | tf_op jit(solution)/shard_map/mlp/pallas_call | solution.py:229
  218.7 119.1 %tail.1 = (bf16[256,2048]{1,0:T(8,128)(2,1)}, bf16[256,2048]{1,0:T(8,128)(2,1)}, f32[8,2048]{1,0:T(8,128)}, bf16[2048,768]{1,0:T(8,128)(2,1)}, bf16[256,2048]{1,0:T(8,128)(2,1)}, /*index=5*/f32[2,3,128]{2,1,0:T(4,128)}) custom-call(f32[2]{0:T(128)} %dynamic_slice.3.sl_ref, bf16[256,2048]{1,0:T(8,128)(2,1)} %get-tuple-element.38.gm_hbm, ...), custom_call_target="tpu_custom_call" | custom-call | flops 59055800320 | bytes 33554432 | tf_op jit(solution)/shard_map/tail/pallas_call | solution.py:229
  337.7 0.0 copy-start.4
  337.8 1.3 copy.30
  339.1 1.7 fusion
  340.7 0.0 copy-start.3
  340.8 7.0 %reshape.69 = bf16[2048,3,2,128]{3,2,1,0:T(2,128)(2,1)} reshape(bf16[2048,768]{1,0:T(8,128)(2,1)} %get-tuple-element.49) | data formatting | bytes 6291456 | tf_op jit(solution)/shard_map/reshape | solution.py:795
  347.8 0.0 copy-done.4
  347.8 1.0 copy.38
  348.8 0.0 copy-done.3
  348.8 1.0 copy.39
  349.7 0.0 copy-done.2
  349.7 1.0 copy.40
  350.7 0.1 copy-done.1
  350.9 2.1 copy.41
  353.0 0.0 copy-done.6
  353.0 0.6 copy.42
  353.6 1.0 copy-done
  354.6 2.0 copy.43
  356.6 0.0 copy-done.5
  356.6 0.6 copy.44
  (5 shorter events, 0.0 us)
Async XLA Ops:
  337.7 10.1 %copy-start.4 = (bf16[256,2048]{1,0:T(8,128)(2,1)S(1)}, bf16[256,2048]{1,0:T(8,128)(2,1)}, u32[]{:S(2)}) copy-start(bf16[256,2048]{1,0:T(8,128)(2,1)} %get-tuple-element.46) | copy-start | bytes 3145732
  340.7 8.0 %copy-start.3 = (bf16[256,2048]{1,0:T(8,128)(2,1)S(1)}, bf16[256,2048]{1,0:T(8,128)(2,1)}, u32[]{:S(2)}) copy-start(bf16[256,2048]{1,0:T(8,128)(2,1)} %get-tuple-element.47) | copy-start | bytes 3145732
  340.8 9.0 %copy-start.2 = (bf16[256,2048]{1,0:T(8,128)(2,1)S(1)}, bf16[256,2048]{1,0:T(8,128)(2,1)}, u32[]{:S(2)}) copy-start(bf16[256,2048]{1,0:T(8,128)(2,1)} %get-tuple-element.95) | copy-start | bytes 3145732
  347.8 3.1 copy-start.1
  350.9 2.1 copy-start.6
  350.9 3.7 %copy-start = (bf16[1024,2048]{1,0:T(8,128)(2,1)S(1)}, bf16[1024,2048]{1,0:T(8,128)(2,1)}, u32[]{:S(2)}) copy-start(bf16[1024,2048]{1,0:T(8,128)(2,1)} %get-tuple-element.101) | copy-start | bytes 12582916
  354.6 2.0 copy-start.5

commit v2 on v1

--- a/solution.py
+++ b/solution.py
@@ -263,35 +263,67 @@
     loop(0, ROWS // RB, lambda i: fn(pl.ds(pl.multiple_of(i * RB, RB), RB)))
 
 
-def front_kernel(sl_ref, x_hbm, g1_ref, b1_ref, w6_hbm, bq_ref, gyl_hbm, wo_hbm, bo_ref, g2_ref, b2_ref,
-                 qkv_out, ctx_out, lse_ref, h_out, gy_out, x1_ref, gl_ref,
-                 full, ss, rs, gyf, ssy, rsy, x, w6, wo, qkv, ctx, bias, biasm, acc, ml, ls, hs, ys, *scratch):
+def front_kernel(sl_ref, x_hbm, g1_ref, b1_ref, wq_hbm, bq_ref, gyl_hbm, wo_hbm, bo_ref, g2_ref, b2_ref, wd_hbm,
+                 qkv_out, ctx_out, lse_ref, h_out, gy_out, x1_ref, gl_ref, w6_out, ga_out, gbd_ref,
+                 full, ss, rs, gyf, ssy, rsy, x, w6, wo, qkv, ctx, bias, biasm, acc, ml, wq, wd, ga, ls, hs, ys, zs, *scratch):
     ag = Gather(full, ss, rs)
     gg = Gather(gyf, ssy, rsy)
     sc = Scatter(*scratch)
-    pairs = [(x_hbm, x), (gyl_hbm, gyf.at[rows_at(ag.me)]), (w6_hbm, w6), (wo_hbm, wo)]
+    pairs = [(gyl_hbm, gyf.at[rows_at(ag.me)]), (x_hbm, x), (wq_hbm, wq), (wd_hbm, wd), (wo_hbm, wo)]
     loads = [pltpu.make_async_copy(src, dst, ls.at[i]) for i, (src, dst) in enumerate(pairs)]
     for l in loads:
         l.start()
+    ag.barrier()
     loads[0].wait()
+    for k in (0, 3, 6):
+        gg.send(k)
+    loads[1].wait()
 
     def ln(i):
         rows = pl.ds(pl.multiple_of(i * RB, RB), RB)
         dst = pl.ds(pl.multiple_of(ag.me * ROWS + i * RB, RB), RB)
         full[dst] = norm_rows(x[rows].astype(F32), g1_ref[...], b1_ref[...]).astype(BF)
     loop(0, ROWS // RB, ln)
-    ag.barrier()
     c1 = (128 ** -0.5) * LOG2E
+
+    def slope(h):
+        return sl_ref[2 * ag.me + h] * LOG2E
 
     def biases():
         ki = lax.broadcasted_iota(jnp.int32, (CHIP, CHIP), 0)
         qi = lax.broadcasted_iota(jnp.int32, (CHIP, CHIP), 1)
         for h in range(2):
-            b = ki.astype(F32) * (sl_ref[h] * LOG2E)
+            b = ki.astype(F32) * slope(h)
             bias[h] = b
             biasm[h] = jnp.where(ki <= qi, b, MASK_VALUE)
-        for l in loads[1:]:
+    biases()
+    chips = [pl.multiple_of((b // 2) * CHIP, CHIP) for b in (ag.me, ag.xn, ag.yn, ag.dg)]
+    gbd_ref[...] = jnp.zeros_like(gbd_ref)
+
+    def act(i):
+        rows = pl.ds(chips[i], CHIP)
+        def body(n):
+            cols = pl.ds(pl.multiple_of(n * 256, 256), 256)
+            ga[rows, cols] = dot_nt(gyf[rows], wd[cols]).astype(BF)
+        loop(0, 4, body)
+        pltpu.make_async_copy(ga.at[rows], ga_out.at[rows], zs.at[i]).start()
+
+    def colsum(n):
+        part = pl.ds(pl.multiple_of(n * RB, RB), RB)
+        gbd_ref[...] += jnp.sum(gyf[part].astype(F32), axis=0, keepdims=True)
+
+    def weights():
+        for l in loads[2:]:
             l.wait()
+        def body(i):
+            part = pl.ds(pl.multiple_of(i * CHIP, CHIP), CHIP)
+            for t in range(3):
+                for h in range(2):
+                    w6[2 * t + h, part] = wq[part, t, h]
+        loop(0, 4, body)
+        pltpu.make_async_copy(w6, w6_out, ls.at[2]).start()
+        gg.recv(6)
+        act(0)
 
     def compute(idx, r0):
         rows = pl.ds(r0, CHIP)
@@ -303,10 +335,17 @@
         loop(0, 3, body)
 
     def start_gy():
-        for k in (0, 3, 1, 4, 6):
-            gg.send(k)
-    ag.run(compute, pre=biases, landed=start_gy)
-    stores = [pltpu.make_async_copy(qkv, qkv_out, ls.at[4]), pltpu.make_async_copy(ctx, ctx_out, ls.at[5])]
+        gg.send(1)
+        gg.send(4)
+        gg.recv(0)
+        gg.send(5)
+        gg.send(7)
+        gg.recv(3)
+        gg.send(2)
+        gg.send(9)
+    ag.run(compute, pre=weights, landed=start_gy)
+    stores = [pltpu.make_async_copy(qkv, qkv_out, ls.at[0]), pltpu.make_async_copy(ctx, ctx_out, ls.at[1]),
+              pltpu.make_async_copy(w6, w6_out, ls.at[2])]
     stores[0].start()
 
     def tile(block, n):
@@ -324,7 +363,7 @@
 
         def one(h):
             lanes = [pl.ds(pl.multiple_of((2 * t + h) * 128, 128), 128) for t in range(3)]
-            sl = sl_ref[h] * LOG2E
+            sl = slope(h)
             q = qkv[qrows, lanes[0]]
             ml[0:1] = jnp.full((1, CHIP), MASK_VALUE, F32)
             ml[1:2] = jnp.zeros((1, CHIP), F32)
@@ -349,12 +388,6 @@
     loop(0, 4, attend)
     stores[1].start()
 
-    gg.recv(0)
-    gg.send(5)
-    gg.send(7)
-    gg.recv(3)
-    gg.send(2)
-    gg.send(9)
     sc.keep(0, tile)
     sc.start(4, 7)
     sc.keep(1, tile)
@@ -367,23 +400,28 @@
     gg.recv(4)
     gg.send(10)
 
-    chips = [pl.multiple_of((b // 2) * CHIP, CHIP) for b in (ag.me, ag.xn, ag.yn, ag.dg)]
     def keep_gy(i):
         rows = pl.ds(chips[i], CHIP)
         return pltpu.make_async_copy(gyf.at[rows], gy_out.at[rows], ys.at[i])
-    gg.recv(6)
     keep_gy(0).start()
-    sc.relays()
-    for k in (7, 8):
-        gg.recv(k)
+    gg.recv(7)
+    gg.recv(8)
     keep_gy(1).start()
-    for k in (9, 10):
-        gg.recv(k)
-    keep_gy(2).start()
+    act(1)
     gg.recv(5)
     gg.send(11)
     gg.recv(2)
     gg.send(12)
+    gg.recv(9)
+    gg.recv(10)
+    keep_gy(2).start()
+    act(2)
+    gg.recv(11)
+    gg.recv(12)
+    keep_gy(3).start()
+    sc.relays()
+    act(3)
+    loop(0, SEQ // RB, colsum)
     sc.arrive()
 
     def fin(rows):
@@ -391,9 +429,6 @@
         x1_ref[rows] = x1
         gl_ref[rows] = norm_rows(x1, g2_ref[...], b2_ref[...]).astype(BF)
     row_blocks(fin)
-    for k in (11, 12):
-        gg.recv(k)
-    keep_gy(3).start()
     sc.finish()
     for k in range(13):
         gg.copy(k, gg.send_rows[k]).wait_send()
@@ -402,24 +437,23 @@
     for i in range(4):
         rows = pl.ds(i * CHIP, CHIP)
         pltpu.make_async_copy(full.at[rows], h_out.at[rows], hs.at[i]).wait()
+        pltpu.make_async_copy(ga.at[rows], ga_out.at[rows], zs.at[i]).wait()
         keep_gy(i).wait()
 
 
-def mlp_kernel(g_hbm, gy_hbm, wu_hbm, bu_ref, wd_hbm, x1_hbm, g2_ref,
-               r_out, gm_ref, gmb_ref, vec_ref, gwu_out, gwd_out, gbu_ref, gbd_ref,
-               full, ss, rs, gy, wu, wd, x1, gp, r, gw, ls, ys, *scratch):
+def mlp_kernel(g_hbm, gy_hbm, wu_hbm, bu_ref, ga_hbm, x1_hbm, g2_ref,
+               r_out, gm_ref, gmb_ref, vec_ref, gwu_out, gwd_out, gbu_ref,
+               full, ss, rs, gy, wu, x1, gp, r, gw, ls, ys, *scratch):
     ag = Gather(full, ss, rs)
     sc = Scatter(*scratch)
     own = pltpu.make_async_copy(g_hbm, full.at[rows_at(ag.me)], ls.at[0])
     own.start()
-    load_wd = pltpu.make_async_copy(wd_hbm, wd, ls.at[1])
-    load_wd.start()
     chips = [pl.multiple_of((b // 2) * CHIP, CHIP) for b in (ag.me, ag.xn, ag.yn, ag.dg)]
-    load_gy = [pltpu.make_async_copy(gy_hbm.at[pl.ds(c, CHIP)], gy.at[pl.ds(c, CHIP)], ys.at[i]) for i, c in enumerate(chips)]
-    for l in load_gy:
-        l.start()
     load_wu = pltpu.make_async_copy(wu_hbm, wu, ls.at[2])
     load_wu.start()
+    load_ga = pltpu.make_async_copy(ga_hbm, gp, ls.at[1])
+    load_ga.start()
+    load_gy = pltpu.make_async_copy(gy_hbm, gy, ys.at[0])
     load_x1 = pltpu.make_async_copy(x1_hbm, x1, ls.at[3])
     load_x1.start()
     own.wait()
@@ -427,20 +461,8 @@
     for k in (0, 3, 1, 4, 6):
         ag.send(k)
     gbu_ref[...] = jnp.zeros_like(gbu_ref)
-    gbd_ref[...] = jnp.zeros_like(gbd_ref)
     vec_ref[...] = jnp.zeros_like(vec_ref)
-
-    def act(i):
-        rows = pl.ds(chips[i], CHIP)
-        load_gy[i].wait()
-        def body(n):
-            cols = pl.ds(pl.multiple_of(n * 256, 256), 256)
-            gp[rows, cols] = dot_nt(gy[rows], wd[cols]).astype(BF)
-        loop(0, 4, body)
-
-    def colsum(n):
-        part = pl.ds(pl.multiple_of(n * RB, RB), RB)
-        gbd_ref[...] += jnp.sum(gy[part].astype(F32), axis=0, keepdims=True)
+    load_gy.start()
 
     k0 = math.sqrt(2.0 / math.pi)
     k1 = 0.044715
@@ -465,21 +487,17 @@
         cols = pl.ds(pl.multiple_of(n * TN, TN), TN)
         return dot_nt(gp[rows_at(block)], wu[cols])
 
-    load_wd.wait()
-    act(0)
     load_wu.wait()
+    load_ga.wait()
+    load_gy.wait()
     ag.recv(6)
     up(0)
-    act(1)
     ag.recv(0)
     ag.send(5)
     ag.send(7)
     ag.recv(3)
     ag.send(2)
     ag.send(9)
-    act(2)
-    act(3)
-    loop(0, SEQ // RB // 2, colsum)
     ag.recv(1)
     ag.send(8)
     ag.recv(4)
@@ -527,7 +545,6 @@
     sc.relays()
     loop(6, 8, gwu_step)
     loop(0, 4, gwd_step)
-    loop(SEQ // RB // 2, SEQ // RB, colsum)
     load_x1.wait()
     sc.arrive()
 
@@ -634,10 +651,10 @@
     def put(h, t, rows, val):
         val = val.astype(BF)
         gq[rows, (2 * t + h) * 128:(2 * t + h + 1) * 128] = val
-        gb_ref[h, t:t + 1] += jnp.sum(val.astype(F32), axis=0, keepdims=True)
+        gb_ref[t, h:h + 1] += jnp.sum(val.astype(F32), axis=0, keepdims=True)
 
     def head(h):
-        sl = sl_ref[h] * LOG2E
+        sl = sl_ref[2 * ag.me + h] * LOG2E
         ki = lax.broadcasted_iota(jnp.int32, (CHIP, CHIP), 0)
         qi = lax.broadcasted_iota(jnp.int32, (CHIP, CHIP), 1)
         b = ki.astype(F32) * sl
@@ -697,7 +714,10 @@
     def wq():
         def body(i):
             src = pl.ds(pl.multiple_of(i * 256, 256), 256)
-            gwq[src] = dot_tn(r[:, src], gq[...]).astype(BF)
+            val = dot_tn(r[:, src], gq[...])
+            for t in range(3):
+                pair = [val[:, (2 * t + h) * 128:(2 * t + h + 1) * 128] for h in range(2)]
+                gwq[src, t] = jnp.stack(pair, axis=1).astype(BF)
         return body
 
     load_h[0].wait()
@@ -755,44 +775,44 @@
 
 def solution(mesh):
     def local_step(x, ln1_gamma, ln1_beta, w_qkv, b_qkv, w_out, b_out, ln2_gamma, ln2_beta, w_up, b_up, w_down, b_down, grad_y):
-        tp_index = lax.axis_index('tp')
-        slopes = lax.dynamic_slice_in_dim(alibi_slopes(16), tp_index * 2, 2)
+        slopes = alibi_slopes(16)
         row = lambda v: v.reshape(1, -1)
         x2, gy2 = x[0], grad_y[0]
-        w6 = w_qkv.transpose(2, 1, 0, 3).reshape(6, D, 128)
         bq = b_qkv.transpose(1, 0, 2).reshape(1, 768)
 
-        qkv, ctx, lse, h_full, gy_full, x1, g_loc = call(
-            front_kernel, 'front', 0, [pl.BlockSpec(memory_space=pltpu.SMEM), HB, VM, VM, HB, VM, HB, HB, VM, VM, VM],
+        qkv, ctx, lse, h_full, gy_full, x1, g_loc, w6, ga, gbd = call(
+            front_kernel, 'front', 0, [pl.BlockSpec(memory_space=pltpu.SMEM), HB, VM, VM, HB, VM, HB, HB, VM, VM, VM, HB],
             [((SEQ, 768), BF, HB), ((SEQ, 256), BF, HB), ((2, 1, SEQ), F32, VM), ((SEQ, D), BF, HB), ((SEQ, D), BF, HB),
-             ((ROWS, D), F32, VM), ((ROWS, D), BF, VM)],
+             ((ROWS, D), F32, VM), ((ROWS, D), BF, VM), ((6, D, 128), BF, HB), ((SEQ, 1024), BF, HB), ((1, D), F32, VM)],
             GATHER_SCRATCH * 2 + [pltpu.VMEM((ROWS, D), BF), pltpu.VMEM((6, D, 128), BF), pltpu.VMEM((256, D), BF),
                                   pltpu.VMEM((SEQ, 768), BF), pltpu.VMEM((SEQ, 256), BF), pltpu.VMEM((2, CHIP, CHIP), F32),
                                   pltpu.VMEM((2, CHIP, CHIP), F32), pltpu.VMEM((128, CHIP), F32), pltpu.VMEM((8, CHIP), F32),
-                                  pltpu.SemaphoreType.DMA((6,)), pltpu.SemaphoreType.DMA((4,)), pltpu.SemaphoreType.DMA((4,))]
+                                  pltpu.VMEM((D, 3, 2, 128), BF), pltpu.VMEM((1024, D), BF), pltpu.VMEM((SEQ, 1024), BF),
+                                  pltpu.SemaphoreType.DMA((5,))] + [pltpu.SemaphoreType.DMA((4,))] * 3
             + SCATTER_SCRATCH,
-            (slopes, x2, row(ln1_gamma), row(ln1_beta), w6, bq, gy2, w_out, row(b_out), row(ln2_gamma), row(ln2_beta)), 12 << 30)
-        r, gm, gm_bf, vec2, g_wu, g_wd, gbu, gbd = call(
+            (slopes, x2, row(ln1_gamma), row(ln1_beta), w_qkv.transpose(0, 2, 1, 3), bq, gy2, w_out, row(b_out), row(ln2_gamma),
+             row(ln2_beta), w_down), 20 << 30)
+        r, gm, gm_bf, vec2, g_wu, g_wd, gbu = call(
             mlp_kernel, 'mlp', 2, [HB, HB, HB, VM, HB, HB, VM],
             [((SEQ, 1024), BF, HB), ((ROWS, D), F32, VM), ((ROWS, D), BF, VM), ((8, D), F32, VM), ((D, 1024), BF, HB),
-             ((1024, D), BF, HB), ((1, 1024), F32, VM), ((1, D), F32, VM)],
-            GATHER_SCRATCH + [pltpu.VMEM((SEQ, D), BF), pltpu.VMEM((D, 1024), BF), pltpu.VMEM((1024, D), BF), pltpu.VMEM((ROWS, D), F32),
+             ((1024, D), BF, HB), ((1, 1024), F32, VM)],
+            GATHER_SCRATCH + [pltpu.VMEM((SEQ, D), BF), pltpu.VMEM((D, 1024), BF), pltpu.VMEM((ROWS, D), F32),
                               pltpu.VMEM((SEQ, 1024), BF), pltpu.VMEM((SEQ, 1024), BF), pltpu.VMEM((256, D), BF),
                               pltpu.SemaphoreType.DMA((5,)), pltpu.SemaphoreType.DMA((4,))] + SCATTER_SCRATCH,
-            (g_loc, gy_full, w_up, row(b_up), w_down, x1, row(ln2_gamma)), 45 << 30)
+            (g_loc, gy_full, w_up, row(b_up), ga, x1, row(ln2_gamma)), 36 << 30)
         y, g_x, vec, g_wq, g_wo, g_bq = call(
             tail_kernel, 'tail', 3, [pl.BlockSpec(memory_space=pltpu.SMEM)] + [HB] * 6 + [VM] + [HB] * 4 + [VM] * 2 + [HB, VM],
-            [((ROWS, D), BF, VM), ((ROWS, D), BF, VM), ((8, D), F32, VM), ((D, 768), BF, HB), ((256, D), BF, HB), ((2, 3, 128), F32, VM)],
+            [((ROWS, D), BF, VM), ((ROWS, D), BF, VM), ((8, D), F32, VM), ((D, 3, 2, 128), BF, HB), ((256, D), BF, HB), ((3, 2, 128), F32, VM)],
             GATHER_SCRATCH + [pltpu.VMEM((256, D), BF), pltpu.VMEM((SEQ, 1024), BF), pltpu.VMEM((1024, D), BF), pltpu.VMEM((SEQ, 768), BF),
                               pltpu.VMEM((SEQ, 256), BF), pltpu.VMEM((6, D, 128), BF), pltpu.VMEM((ROWS, D), F32),
-                              pltpu.VMEM((SEQ, 256), BF), pltpu.VMEM((SEQ, 768), BF), pltpu.VMEM((1024, 768), BF),
+                              pltpu.VMEM((SEQ, 256), BF), pltpu.VMEM((SEQ, 768), BF), pltpu.VMEM((1024, 3, 2, 128), BF),
                               pltpu.VMEM((256, D), BF), pltpu.VMEM((CHIP, CHIP), F32), pltpu.VMEM((CHIP, CHIP), F32),
                               pltpu.VMEM((2, SEQ), F32), pltpu.VMEM((128, SEQ), F32), pltpu.VMEM((CHIP, 128), F32),
                               pltpu.VMEM((CHIP, 128), F32), pltpu.VMEM((8, D), F32), pltpu.VMEM((8, 8, D), F32),
                               pltpu.SemaphoreType.DMA((14,)), pltpu.SemaphoreType.DMA((7,)), pltpu.SemaphoreType.DMA((7,))]
             + SCATTER_SCRATCH + SCATTER_REST,
             (slopes, gm_bf, w_out, r, w_down, qkv, ctx, lse, w6, x2, gm, x1, row(b_down), row(ln1_gamma), h_full, vec2), 55 << 30)
-        g_wq = g_wq.reshape(D, 3, 2, 128).transpose(0, 2, 1, 3)
+        g_wq, g_bq = g_wq.transpose(0, 2, 1, 3), g_bq.transpose(1, 0, 2)
         return (y[None], g_x[None], vec[3], vec[4], g_wq, g_bq, g_wo, vec[2], vec[0], vec[1], g_wu, gbu[0], g_wd, gbd[0])
 
     row_spec = P('dp', 'tp', None)

time: 358 us -> 345 us (0.964)
  local copies, waits for them, and re-layouts: 24.6 us -> 16.4 us
  Pallas kernels: 332 us -> 327 us
    reshape x1 -> x0, local copies, waits for them, and re-layouts: 7.04 us -> none  [local_step(): g_wq = g_wq.reshape(D, 3, 2, 128).transpose(0, 2, 1, 3)]
    pallas_call x3, Pallas kernels: 332 us -> 327 us  [call(): pl.pallas_call(body, name=name, out_shape=[jax.ShapeDtypeStruct(s, t) for...]
    transpose x1 -> x0, local copies, waits for them, and re-layouts: 3.96 us -> none  [local_step(): w6 = w_qkv.transpose(2, 1, 0, 3).reshape(6, D, 128)]
    unnamed x22 -> x23, local copies, waits for them, and re-layouts: 10.7 us -> 14.7 us
where the time goes in v2:
time: 345 us
  Pallas kernels  327 us (95%)
  local copies, waits for them, and re-layouts  16.4 us (5%)
    pallas_call x3, Pallas kernels, call(): pl.pallas_call(body, name=name, out_shape=[jax.ShapeDtypeStruct(s, t) for...  327 us
    unnamed x23, local copies, waits for them, and re-layouts  14.7 us

profile of v2, /device:TPU:0, one launch (start us, length us, event | category | flops | bytes accessed | tf_op | source)
XLA Modules:
  0.0 344.6 jit_solution(16193870737545397213)
XLA Ops:
  0.6 114.3 %front.1 = (bf16[2048,768]{1,0:T(8,128)(2,1)}, bf16[2048,256]{1,0:T(8,128)(2,1)}, f32[2,1,2048]{2,1,0:T(1,128)}, bf16[2048,2048]{1,0:T(8,128)(2,1)}, bf16[2048,2...) custom-call(f32[16]{0:T(128)} %constant.2.clone.sl_ref, ...), custom_call_target="tpu_custom_call" | custom-call | flops 21474836480 | bytes 33554432 | tf_op jit(solution)/shard_map/front/pallas_call | solution.py:229
  115.0 94.0 %mlp.1 = (bf16[2048,1024]{1,0:T(8,128)(2,1)}, f32[256,2048]{1,0:T(8,128)}, bf16[256,2048]{1,0:T(8,128)(2,1)}, f32[8,2048]{1,0:T(8,128)}, bf16[2048,1024]{1,0:T(8...) custom-call(bf16[256,2048]{1,0:T(8,128)(2,1)} %get-tuple-element.37.g_hbm, ...), custom_call_target="tpu_custom_call" | custom-call | flops 38654705664 | bytes 33554432 | tf_op jit(solution)/shard_map/mlp/pallas_call | solution.py:229
  209.0 119.1 %tail.1 = (bf16[256,2048]{1,0:T(8,128)(2,1)}, bf16[256,2048]{1,0:T(8,128)(2,1)}, f32[8,2048]{1,0:T(8,128)}, bf16[2048,3,2,128]{3,2,1,0:T(2,128)(2,1)}, bf16[256,2048]{1,0:T(8,128)(2,1)}, /*index=5*/f32[3,2,128]{2,1,0:T(2,128)}) custom-call(f32[16]{0:T(128)} %constant.2.clone.sl_ref, bf16[256,2048]{1,0:T(8,128)(2,1)} %get-tuple-element.41.gm_hbm, ...), custom_call_target="tpu_custom_call" | custom-call | flops 59055800320 | bytes 33554432 | tf_op jit(solution)/shard_map/tail/pallas_call | solution.py:229
  328.1 0.0 copy-start.2
  328.1 1.8 fusion
  329.9 2.3 copy.38
  332.2 0.0 copy-start.6
  332.2 0.0 copy-start.3
  332.2 2.4 copy.39
  334.6 0.0 copy-done.2
  334.6 0.0 copy-start.1
  334.6 1.7 copy.40
  336.2 0.0 copy-done.6
  336.2 0.6 copy.41
  336.8 0.0 copy-done.3
  336.8 1.0 copy.42
  337.8 0.4 copy-done.1
  338.2 2.1 copy.43
  340.4 0.0 copy-done.5
  340.4 0.6 copy.44
  341.0 1.0 copy-done
  341.9 2.0 copy.45
  343.9 0.0 copy-done.4
  343.9 0.6 copy.46
  (3 shorter events, 0.0 us)
Async XLA Ops:
  328.1 6.5 %copy-start.2 = (bf16[2048,3,2,128]{3,2,1,0:T(2,128)(2,1)S(1)}, bf16[2048,3,2,128]{3,2,1,0:T(2,128)(2,1)}, u32[]{:S(2)}) copy-start(bf16[2048,3,2,128]{3,2,1,0:T(2,128)(2,1)} %get-tuple-element.53) | copy-start | bytes 9437188
  332.2 4.1 %copy-start.6 = (f32[3,2,128]{2,1,0:T(2,128)S(1)}, f32[3,2,128]{2,1,0:T(2,128)}, u32[]{:S(2)}) copy-start(f32[3,2,128]{2,1,0:T(2,128)} %get-tuple-element.54) | copy-start | bytes 9220
  332.2 4.6 %copy-start.3 = (bf16[256,2048]{1,0:T(8,128)(2,1)S(1)}, bf16[256,2048]{1,0:T(8,128)(2,1)}, u32[]{:S(2)}) copy-start(bf16[256,2048]{1,0:T(8,128)(2,1)} %get-tuple-element.85) | copy-start | bytes 3145732
  334.6 3.7 %copy-start.1 = (bf16[2048,1024]{1,0:T(8,128)(2,1)S(1)}, bf16[2048,1024]{1,0:T(8,128)(2,1)}, u32[]{:S(2)}) copy-start(bf16[2048,1024]{1,0:T(8,128)(2,1)} %get-tuple-element.89) | copy-start | bytes 12582916
  338.2 2.1 copy-start.5
  338.2 3.7 %copy-start = (bf16[1024,2048]{1,0:T(8,128)(2,1)S(1)}, bf16[1024,2048]{1,0:T(8,128)(2,1)}, u32[]{:S(2)}) copy-start(bf16[1024,2048]{1,0:T(8,128)(2,1)} %get-tuple-element.91) | copy-start | bytes 12582916
  341.9 2.0 copy-start.4

commit v3 on v2

--- a/solution.py
+++ b/solution.py
@@ -271,13 +271,15 @@
     sc = Scatter(*scratch)
     pairs = [(gyl_hbm, gyf.at[rows_at(ag.me)]), (x_hbm, x), (wq_hbm, wq), (wd_hbm, wd), (wo_hbm, wo)]
     loads = [pltpu.make_async_copy(src, dst, ls.at[i]) for i, (src, dst) in enumerate(pairs)]
-    for l in loads:
+    for l in loads[:2]:
         l.start()
     ag.barrier()
     loads[0].wait()
     for k in (0, 3, 6):
         gg.send(k)
     loads[1].wait()
+    for l in loads[2:]:
+        l.start()
 
     def ln(i):
         rows = pl.ds(pl.multiple_of(i * RB, RB), RB)
@@ -443,45 +445,65 @@
 
 def mlp_kernel(g_hbm, gy_hbm, wu_hbm, bu_ref, ga_hbm, x1_hbm, g2_ref,
                r_out, gm_ref, gmb_ref, vec_ref, gwu_out, gwd_out, gbu_ref,
-               full, ss, rs, gy, wu, x1, gp, r, gw, ls, ys, *scratch):
+               full, ss, rs, gy, wu, x1, gp, r, gwu, gwd, ls, ys, *scratch):
     ag = Gather(full, ss, rs)
     sc = Scatter(*scratch)
     own = pltpu.make_async_copy(g_hbm, full.at[rows_at(ag.me)], ls.at[0])
     own.start()
     chips = [pl.multiple_of((b // 2) * CHIP, CHIP) for b in (ag.me, ag.xn, ag.yn, ag.dg)]
     load_wu = pltpu.make_async_copy(wu_hbm, wu, ls.at[2])
-    load_wu.start()
     load_ga = pltpu.make_async_copy(ga_hbm, gp, ls.at[1])
-    load_ga.start()
     load_gy = pltpu.make_async_copy(gy_hbm, gy, ys.at[0])
     load_x1 = pltpu.make_async_copy(x1_hbm, x1, ls.at[3])
-    load_x1.start()
+    ag.barrier()
     own.wait()
-    ag.barrier()
     for k in (0, 3, 1, 4, 6):
         ag.send(k)
+    load_wu.start()
+    load_ga.start()
     gbu_ref[...] = jnp.zeros_like(gbu_ref)
     vec_ref[...] = jnp.zeros_like(vec_ref)
     load_gy.start()
+    load_x1.start()
 
     k0 = math.sqrt(2.0 / math.pi)
     k1 = 0.044715
+
+    def activation(z, grad):
+        z2 = z * z
+        t = jnp.tanh(k0 * (z + k1 * (z2 * z)))
+        half = 0.5 * (1.0 + t)
+        dz = half + (0.5 * z) * (1.0 - t * t) * (k0 * (1.0 + 3.0 * k1 * z2))
+        return z * half, grad * dz
+
+    def store_r(i):
+        rows = pl.ds(chips[i], CHIP)
+        return pltpu.make_async_copy(r.at[rows], r_out.at[rows], ys.at[i])
 
     def up(i):
         rows = pl.ds(chips[i], CHIP)
         def body(n):
             cols = pl.ds(pl.multiple_of(n * 256, 256), 256)
-            z = dot(full[rows], wu[:, cols]) + bu_ref[:, cols]
-            z2 = z * z
-            t = jnp.tanh(k0 * (z + k1 * (z2 * z)))
-            half = 0.5 * (1.0 + t)
-            r[rows, cols] = (z * half).astype(BF)
-            dz = half + (0.5 * z) * (1.0 - t * t) * (k0 * (1.0 + 3.0 * k1 * z2))
-            gpre = gp[rows, cols].astype(F32) * dz
+            act, gpre = activation(dot(full[rows], wu[:, cols]) + bu_ref[:, cols], gp[rows, cols].astype(F32))
+            r[rows, cols] = act.astype(BF)
             gbu_ref[:, cols] += jnp.sum(gpre, axis=0, keepdims=True)
             gp[rows, cols] = gpre.astype(BF)
         loop(0, 4, body)
-        pltpu.make_async_copy(r.at[rows], r_out.at[rows], ys.at[i]).start()
+        store_r(i).start()
+
+    def up_half(block, half):
+        parts = [rows_at(block, half), rows_at(block + sc.delta, half)]
+        def body(n):
+            cols = pl.ds(pl.multiple_of(n * 256, 256), 256)
+            lhs = jnp.concatenate([full[p] for p in parts], axis=0)
+            grad = jnp.concatenate([gp[p, cols] for p in parts], axis=0)
+            act, gpre = activation(dot(lhs, wu[:, cols]) + bu_ref[:, cols], grad.astype(F32))
+            gbu_ref[:, cols] += jnp.sum(gpre, axis=0, keepdims=True)
+            act, gpre = act.astype(BF), gpre.astype(BF)
+            for k, p in enumerate(parts):
+                r[p, cols] = act[k * 128:(k + 1) * 128]
+                gp[p, cols] = gpre[k * 128:(k + 1) * 128]
+        loop(0, 4, body)
 
     def tile(block, n):
         cols = pl.ds(pl.multiple_of(n * TN, TN), TN)
@@ -498,24 +520,28 @@
     ag.recv(3)
     ag.send(2)
     ag.send(9)
+    ag.recv(7)
+    up_half(ag.xn, 0)
+    ag.recv(9)
+    up_half(ag.yn, 1)
     ag.recv(1)
     ag.send(8)
     ag.recv(4)
     ag.send(10)
-    ag.recv(7)
     ag.recv(8)
-    up(1)
+    up_half(ag.xn, 1)
+    store_r(1).start()
     sc.give(1, tile)
-    ag.recv(9)
     ag.recv(10)
-    up(2)
+    up_half(ag.yn, 0)
+    store_r(2).start()
+    sc.keep(1, tile)
+    sc.start(5)
     sc.give(2, tile)
     ag.recv(5)
     ag.send(11)
     ag.recv(2)
     ag.send(12)
-    sc.keep(1, tile)
-    sc.start(5)
     sc.keep(2, tile)
     sc.start(8)
     ag.recv(11)
@@ -529,21 +555,17 @@
 
     def gwu_step(i):
         cols = pl.ds(pl.multiple_of(i * 256, 256), 256)
-        gw[:, pl.ds(0, 1024)] = dot_tn(full[:, cols], gp[...]).astype(BF)
-        c = pltpu.make_async_copy(gw.at[:, pl.ds(0, 1024)], gwu_out.at[cols], ls.at[4])
-        c.start()
-        c.wait()
+        gwu[cols] = dot_tn(full[:, cols], gp[...]).astype(BF)
+        pltpu.make_async_copy(gwu.at[cols], gwu_out.at[cols], ls.at[4]).start()
 
     def gwd_step(i):
         cols = pl.ds(pl.multiple_of(i * 256, 256), 256)
-        gw[...] = dot_tn(r[:, cols], gy[...]).astype(BF)
-        c = pltpu.make_async_copy(gw, gwd_out.at[cols], ls.at[4])
-        c.start()
-        c.wait()
-
-    loop(0, 6, gwu_step)
+        gwd[cols] = dot_tn(r[:, cols], gy[...]).astype(BF)
+        pltpu.make_async_copy(gwd.at[cols], gwd_out.at[cols], ls.at[5]).start()
+
+    loop(0, 7, gwu_step)
     sc.relays()
-    loop(6, 8, gwu_step)
+    loop(7, 8, gwu_step)
     loop(0, 4, gwd_step)
     load_x1.wait()
     sc.arrive()
@@ -565,6 +587,8 @@
     for i in range(4):
         rows = pl.ds(chips[i], CHIP)
         pltpu.make_async_copy(r.at[rows], r_out.at[rows], ys.at[i]).wait()
+    pltpu.make_async_copy(gwu, gwu_out, ls.at[4]).wait()
+    pltpu.make_async_copy(gwd, gwd_out, ls.at[5]).wait()
 
 
 def tail_kernel(sl_ref, gm_hbm, wo_hbm, r_hbm, wd_hbm, qkv_hbm, ctx_hbm, lse_ref, w6_hbm, x_hbm, gmf_hbm, x1_hbm, bd_ref, g1_ref,
@@ -577,13 +601,14 @@
     pairs = [(gm_hbm, full.at[rows_at(ag.me)]), (wd_hbm, wd), (r_hbm, r), (wo_hbm, wo), (qkv_hbm, qkv), (ctx_hbm, ctx), (w6_hbm, w6),
              (x1_hbm, x1)]
     loads = [pltpu.make_async_copy(src, dst, ls.at[i]) for i, (src, dst) in enumerate(pairs)]
-    for l in loads:
-        l.start()
-    loads[0].wait()
+    loads[0].start()
     peers = [lax.rem(ag.me + k, 8) for k in range(1, 8)]
     entry_barrier(peers)
+    loads[0].wait()
     for k in (0, 3, 1, 4, 6):
         ag.send(k)
+    for l in loads[1:]:
+        l.start()
     scale = 128 ** -0.5
     c1 = scale * LOG2E
     vec[...] = vec2_ref[...]
@@ -773,6 +798,44 @@
     vec_out[...] = total
 
 
+def finish_kernel(y, gx, wo, wq, wu, wd, vec, bu, bd, bq, y_out, gx_out, wo_out, wq_out, wu_out, wd_out,
+                  v0, v1, v2, v3, v4, bu_out, bd_out, bq_out, *scratch):
+    bufs, si, so = scratch[:6], scratch[6], scratch[7]
+    parts = []
+    for src, dst, buf, size, n in ((wu, wu_out, bufs[4], 512, 4), (wd, wd_out, bufs[5], 256, 4), (wq, wq_out, bufs[3], 512, 4),
+                                   (y, y_out, bufs[0], 256, 1), (gx, gx_out, bufs[1], 256, 1), (wo, wo_out, bufs[2], 256, 1)):
+        for i in range(n):
+            rows = pl.ds(i * size, size)
+            k = len(parts)
+            parts.append((pltpu.make_async_copy(src.at[rows], buf.at[rows], si.at[k]),
+                          pltpu.make_async_copy(buf.at[rows], dst.at[rows], so.at[k])))
+    for load, _ in parts:
+        load.start()
+    for i, out in enumerate((v0, v1, v2, v3, v4)):
+        out[...] = vec[i:i + 1]
+    bu_out[...] = bu[...]
+    bd_out[...] = bd[...]
+    bq_out[...] = bq[...]
+    for load, store in parts:
+        load.wait()
+        store.start()
+    for _, store in parts:
+        store.wait()
+
+
+def finish(big, small):
+    row = jax.ShapeDtypeStruct((1, D), F32)
+    like = [jax.ShapeDtypeStruct(v.shape, v.dtype) for v in (*big, *small)]
+    return pl.pallas_call(
+        finish_kernel,
+        name='finish',
+        out_shape=like[:6] + [row] * 5 + like[7:],
+        in_specs=[HB] * 6 + [VM] * 4,
+        out_specs=[HB] * 6 + [VM] * 8,
+        scratch_shapes=[pltpu.VMEM(v.shape, BF) for v in big] + [pltpu.SemaphoreType.DMA((15,))] * 2,
+    )(*big, *small)
+
+
 def solution(mesh):
     def local_step(x, ln1_gamma, ln1_beta, w_qkv, b_qkv, w_out, b_out, ln2_gamma, ln2_beta, w_up, b_up, w_down, b_down, grad_y):
         slopes = alibi_slopes(16)
@@ -797,8 +860,8 @@
             [((SEQ, 1024), BF, HB), ((ROWS, D), F32, VM), ((ROWS, D), BF, VM), ((8, D), F32, VM), ((D, 1024), BF, HB),
              ((1024, D), BF, HB), ((1, 1024), F32, VM)],
             GATHER_SCRATCH + [pltpu.VMEM((SEQ, D), BF), pltpu.VMEM((D, 1024), BF), pltpu.VMEM((ROWS, D), F32),
-                              pltpu.VMEM((SEQ, 1024), BF), pltpu.VMEM((SEQ, 1024), BF), pltpu.VMEM((256, D), BF),
-                              pltpu.SemaphoreType.DMA((5,)), pltpu.SemaphoreType.DMA((4,))] + SCATTER_SCRATCH,
+                              pltpu.VMEM((SEQ, 1024), BF), pltpu.VMEM((SEQ, 1024), BF), pltpu.VMEM((D, 1024), BF),
+                              pltpu.VMEM((1024, D), BF), pltpu.SemaphoreType.DMA((6,)), pltpu.SemaphoreType.DMA((4,))] + SCATTER_SCRATCH,
             (g_loc, gy_full, w_up, row(b_up), ga, x1, row(ln2_gamma)), 36 << 30)
         y, g_x, vec, g_wq, g_wo, g_bq = call(
             tail_kernel, 'tail', 3, [pl.BlockSpec(memory_space=pltpu.SMEM)] + [HB] * 6 + [VM] + [HB] * 4 + [VM] * 2 + [HB, VM],
@@ -812,8 +875,10 @@
                               pltpu.SemaphoreType.DMA((14,)), pltpu.SemaphoreType.DMA((7,)), pltpu.SemaphoreType.DMA((7,))]
             + SCATTER_SCRATCH + SCATTER_REST,
             (slopes, gm_bf, w_out, r, w_down, qkv, ctx, lse, w6, x2, gm, x1, row(b_down), row(ln1_gamma), h_full, vec2), 55 << 30)
+        y, g_x, g_wo, g_wq, g_wu, g_wd, g_g2, g_b2, g_bo, g_g1, g_b1, gbu, gbd, g_bq = finish(
+            (y, g_x, g_wo, g_wq, g_wu, g_wd), (vec, gbu, gbd, g_bq))
         g_wq, g_bq = g_wq.transpose(0, 2, 1, 3), g_bq.transpose(1, 0, 2)
-        return (y[None], g_x[None], vec[3], vec[4], g_wq, g_bq, g_wo, vec[2], vec[0], vec[1], g_wu, gbu[0], g_wd, gbd[0])
+        return (y[None], g_x[None], g_g1[0], g_b1[0], g_wq, g_bq, g_wo, g_bo[0], g_g2[0], g_b2[0], g_wu, gbu[0], g_wd, gbd[0])
 
     row_spec = P('dp', 'tp', None)
     in_specs = (row_spec, P(), P(), P(None, 'tp', None, None), P('tp', None, None), P('tp', None), P(), P(), P(),

time: 345 us -> 332 us (0.962)
  local copies, waits for them, and re-layouts: 16.4 us -> 0 us
  Pallas kernels: 327 us -> 331 us
    unnamed x23 -> x0, local copies, waits for them, and re-layouts: 14.7 us -> none
    pallas_call x0 -> x1, Pallas kernels: none -> 12.3 us  [finish(): pl.pallas_call(finish_kernel, name='finish', out_shape=like[:6] + [row] *...]
    pallas_call x3, Pallas kernels: 327 us -> 319 us  [call(): pl.pallas_call(body, name=name, out_shape=[jax.ShapeDtypeStruct(s, t) for...]
where the time goes in v3:
time: 332 us
  Pallas kernels  331 us (100%)
    pallas_call x3, Pallas kernels, call(): pl.pallas_call(body, name=name, out_shape=[jax.ShapeDtypeStruct(s, t) for...  319 us
    pallas_call x1, Pallas kernels, finish(): pl.pallas_call(finish_kernel, name='finish', out_shape=like[:6] + [row] *...  12.3 us

profile of v3, /device:TPU:0, one launch (start us, length us, event | category | flops | bytes accessed | tf_op | source)
XLA Modules:
  0.0 331.9 jit_solution(10498141288330079002)
XLA Ops:
  0.6 114.3 %front.1 = (bf16[2048,768]{1,0:T(8,128)(2,1)}, bf16[2048,256]{1,0:T(8,128)(2,1)}, f32[2,1,2048]{2,1,0:T(1,128)}, bf16[2048,2048]{1,0:T(8,128)(2,1)}, bf16[2048,2...) custom-call(f32[16]{0:T(128)} %constant.2.clone.sl_ref, ...), custom_call_target="tpu_custom_call" | custom-call | flops 21474836480 | bytes 33554432 | tf_op jit(solution)/shard_map/front/pallas_call | solution.py:229
  115.0 86.2 %mlp.1 = (bf16[2048,1024]{1,0:T(8,128)(2,1)}, f32[256,2048]{1,0:T(8,128)}, bf16[256,2048]{1,0:T(8,128)(2,1)}, f32[8,2048]{1,0:T(8,128)}, bf16[2048,1024]{1,0:T(8...) custom-call(bf16[256,2048]{1,0:T(8,128)(2,1)} %get-tuple-element.51.g_hbm, ...), custom_call_target="tpu_custom_call" | custom-call | flops 38654705664 | bytes 33554432 | tf_op jit(solution)/shard_map/mlp/pallas_call | solution.py:229
  201.2 118.2 %tail.1 = (bf16[256,2048]{1,0:T(8,128)(2,1)}, bf16[256,2048]{1,0:T(8,128)(2,1)}, f32[8,2048]{1,0:T(8,128)}, bf16[2048,3,2,128]{3,2,1,0:T(2,128)(2,1)}, bf16[256,2048]{1,0:T(8,128)(2,1)}, /*index=5*/f32[3,2,128]{2,1,0:T(2,128)}) custom-call(f32[16]{0:T(128)} %constant.2.clone.sl_ref, bf16[256,2048]{1,0:T(8,128)(2,1)} %get-tuple-element.55.gm_hbm, ...), custom_call_target="tpu_custom_call" | custom-call | flops 59055800320 | bytes 33554432 | tf_op jit(solution)/shard_map/tail/pallas_call | solution.py:229
  319.4 12.3 %finish.1 = (bf16[256,2048]{1,0:T(8,128)(2,1)}, bf16[256,2048]{1,0:T(8,128)(2,1)}, bf16[256,2048]{1,0:T(8,128)(2,1)}, bf16[2048,3,2,128]{3,2,1,0:T(2,128)(2,1)},...) custom-call(bf16[256,2048]{1,0:T(8,128)(2,1)} %get-tuple-element.64., ...), custom_call_target="tpu_custom_call" | custom-call | tf_op jit(solution)/shard_map/finish/pallas_call | solution.py:829
